TPU v7x, 512 devices: a 8x2x16 block of a 8x8x16 slice. The times are simulated.
512 devices in a mesh: groups: 2 (over y), seg: 32 (over z, core), bin: 8 (over x).
Axes of the slice: x: 8, y: 2, z: 16, core: 2. Of those that a mesh axis runs over, the one named last changes fastest.
The devices are a block of a 8x8x16 slice.
Arguments:
- start_factors: float32 [32768, 128], P(('groups', 'seg', 'bin')), parts along dimension 0, may hold values from -6 to 6
- bin_factors: bfloat16 [16384, 128], P(('groups', 'bin')), parts along dimension 0, may hold values from -0.5 to 0.5
- tile_speed: bfloat16 [64, 8, 12, 128, 128], P(('groups', 'seg'), 'bin'), parts along dimension 0, may hold values from -6 to 6
- tile_weight: bfloat16 [64, 8, 12, 128, 128], P(('groups', 'seg'), 'bin'), parts along dimension 0, may hold values from 0.099609375 to 2
- tile_cells: int32 [64, 8, 12, 2], P(('groups', 'seg'), 'bin'), parts along dimension 0, may hold values from 0 to 7, as said below
- tile_count: int32 [64, 8], P(('groups', 'seg'), 'bin'), parts along dimension 0, may hold values from 1 to 12, as said below
- inner_pairs: int32 [64, 8, 2, 2], P(('groups', 'seg'), 'bin'), parts along dimension 0, may hold values from 0 to 3, as said below
- inner_weight: float32 [64, 8, 2, 128, 128], P(('groups', 'seg'), 'bin'), parts along dimension 0, may hold values from 0 to 0.00390625
- face_rows: int32 [64, 8, 2, 256], P(('groups', 'seg'), 'bin'), parts along dimension 0, may hold values from 0 to 511, as said below
- face_count: int32 [64, 8, 2], P(('groups', 'seg'), 'bin'), parts along dimension 0, may hold values from 128 to 256, as said below
- face_weight: float32 [64, 8, 256, 256], P(('groups', 'seg'), 'bin'), parts along dimension 0, may hold values from 0 to 0.00390625
Outputs:
- solution_factors: float32 [32768, 128], P(('groups', 'seg', 'bin')), parts along dimension 0
- residual: float32 [32768, 128], P(('groups', 'seg', 'bin')), parts along dimension 0
There are 2 independent parts, one for each index of `groups`. A program takes and returns all parts, laid end to end along the dimension named above; each array names one. Nothing has to cross between parts.
Inputs may be any that keep to these rules, and one draw needn't show every extreme that they name: `tile_cells`: the 12 slots of one device name different pairs; the first entry is a segment block of the partition, the second a bin block of the device's bins. `tile_count`: some device of every draw has all 12 slots live. `inner_pairs`: the two blocks of a pair differ; both are segment blocks of the partition. `face_rows`: row numbers within the partition, different within each face list. `face_count`: some face list of every draw has all 256 rows live.
All inputs are finite; a program needn't handle non-finite values.
Results may differ from a plain program's by a relative error of at most 0.0024.
Values sent between devices are 32-bit elements; how exact they have to be, the bound alone decides.
A program may use at most 64 MiB of HBM per device.

v0:
```python
import jax
import jax.numpy as jnp
from jax import lax
from jax.sharding import Mesh
from jax.sharding import PartitionSpec as P

ITERS = 2
SEG = ("seg_0", "seg_1")
SEG_BIN = ("seg_0", "seg_1", "bin")
GROUPS_SEG_BIN = ("groups", "seg_0", "seg_1", "bin")
GROUPS_SEG = ("groups", "seg_0", "seg_1")


highest = lax.Precision.HIGHEST
ridge_weight = 0.5


def from_behind(x, axis, by):
    devices = lax.axis_size(axis)
    pairs = [(i, i + by) for i in range(devices) if 0 <= i + by < devices]
    return lax.ppermute(x, axis, pairs)


def cut_along(x, dim, devices):
    before, after = (x.shape[:dim], x.shape[dim + 1 :])
    return jnp.moveaxis(x.reshape(*before, devices, -1, *after), dim, 0)


def sent_and_summed(x, axis, dim):
    devices = lax.axis_size(axis)
    blocks = lax.all_to_all(cut_along(x, dim, devices), axis, 0, 0, tiled=True)
    return jnp.sum(blocks, axis=0)


def in_order(blocks, dim):
    shape = list(blocks.shape[1:])
    shape[dim] *= blocks.shape[0]
    return jnp.moveaxis(blocks, 0, dim).reshape(shape)


def sent_to_all(x, axis):
    devices = lax.axis_size(axis)
    return lax.all_to_all(jnp.broadcast_to(x[None], (devices, *x.shape)), axis, 0, 0, tiled=True)


def gathered_copies(x, axis, dim):
    return in_order(sent_to_all(x, axis), dim)


def one_axis_at_a_time(x, axes):
    for axis in axes:
        x = lax.psum(x, axis)
    return x


def shards(
    start_factors,
    bin_factors,
    tile_speed,
    tile_weight,
    tile_cells,
    tile_count,
    inner_pairs,
    inner_weight,
    face_rows,
    face_count,
    face_weight,
):
    speeds = tile_speed[0, 0]
    weights = tile_weight[0, 0]
    cells = tile_cells[0, 0]
    n_tiles = speeds.shape[0]
    tile_size = speeds.shape[1]
    own_rows = start_factors.shape[0]
    width = start_factors.shape[1]
    part_rows = own_rows * lax.axis_size("bin")
    part_blocks = part_rows // tile_size
    block_ids = jnp.arange(part_blocks, dtype=jnp.int32)
    live_tiles = (jnp.arange(n_tiles, dtype=jnp.int32) < tile_count[0, 0]).astype(jnp.float32)
    tile_bins = bin_factors.reshape(-1, tile_size, width)[cells[:, 1]]
    bins_wide = tile_bins.astype(jnp.float32)
    tile_gain = weights.astype(jnp.float32) * live_tiles[:, None, None]
    tile_onehot = (cells[:, 0][:, None] == block_ids[None, :]).astype(jnp.float32)
    weighted = (weights.astype(jnp.float32) * speeds.astype(jnp.float32)).astype(jnp.bfloat16)
    rhs_terms = jnp.einsum("kij,kjr->kir", weighted, tile_bins, preferred_element_type=jnp.float32)
    rhs_terms = rhs_terms * live_tiles[:, None, None]
    rhs_part = jnp.einsum("kb,kir->bir", tile_onehot, rhs_terms, precision=highest).reshape(
        part_rows, width
    )
    pairs = inner_pairs[0, 0]
    pair_weight = inner_weight[0, 0]
    left_onehot = (pairs[:, 0][:, None] == block_ids[None, :]).astype(jnp.float32)
    right_onehot = (pairs[:, 1][:, None] == block_ids[None, :]).astype(jnp.float32)
    left_degree = pair_weight.sum(2)
    right_degree = pair_weight.sum(1)
    rows_low = face_rows[0, 0, 0]
    rows_up = face_rows[0, 0, 1]
    face_slots = jnp.arange(rows_low.shape[0], dtype=jnp.int32)
    mask_low = (face_slots < face_count[0, 0, 0]).astype(jnp.float32)
    mask_up = (face_slots < face_count[0, 0, 1]).astype(jnp.float32)
    upper_count = face_count[0, 0, 1:2]
    face_block = face_weight[0, 0]

    def apply_local(whole_rows):
        blocks = whole_rows.reshape(part_blocks, tile_size, width)
        picked = blocks[cells[:, 0]]
        scores = jnp.einsum("kir,kjr->kij", picked, bins_wide, precision=highest) * tile_gain
        pulled = jnp.einsum("kij,kjr->kir", scores, bins_wide, precision=highest)
        left = blocks[pairs[:, 0]]
        right = blocks[pairs[:, 1]]
        to_left = left_degree[..., None] * left - jnp.einsum(
            "kij,kjr->kir", pair_weight, right, precision=highest
        )
        to_right = right_degree[..., None] * right - jnp.einsum(
            "kij,kir->kjr", pair_weight, left, precision=highest
        )
        summed = jnp.einsum("kb,kir->bir", tile_onehot, pulled, precision=highest)
        summed = summed + jnp.einsum("kb,kir->bir", left_onehot, to_left, precision=highest)
        summed = summed + jnp.einsum("kb,kir->bir", right_onehot, to_right, precision=highest)
        summed = summed.reshape(part_rows, width)
        own_face = whole_rows[rows_low] * mask_low[:, None]
        upper_face = whole_rows[rows_up] * mask_up[:, None]
        lower_face, lower_count = from_behind((upper_face, upper_count), SEG, 1)
        lower_mask = (face_slots < lower_count[0]).astype(jnp.float32)
        coupling = face_block * mask_low[:, None] * lower_mask[None, :]
        own_term = coupling.sum(1)[:, None] * own_face - jnp.dot(
            coupling, lower_face, precision=highest
        )
        answer = coupling.sum(0)[:, None] * lower_face - jnp.dot(
            coupling.T, own_face, precision=highest
        )
        returned = from_behind(answer, SEG, -1)
        return summed.at[rows_low].add(own_term).at[rows_up].add(returned)

    def reduce_rows(partial_value):
        reduced = sent_and_summed(partial_value, "bin", 0)
        return reduced

    def spread(vector):
        whole_rows = gathered_copies(vector, "bin", 0)
        return whole_rows

    def fold_sum(values):
        folded = (one_axis_at_a_time(values[0], SEG_BIN), one_axis_at_a_time(values[1], SEG_BIN))
        return folded

    def image_of(vector):
        return reduce_rows(apply_local(spread(vector))) + ridge_weight * vector

    start_whole = gathered_copies(start_factors, "bin", 0)
    residual = reduce_rows(rhs_part - apply_local(start_whole)) - ridge_weight * start_factors
    solution = start_factors
    images = image_of(residual)
    norm_now, product = fold_sum((jnp.sum(residual * residual), jnp.sum(residual * images)))
    step_size = norm_now / product
    direction = residual
    along = images
    for iteration in range(ITERS):
        solution = solution + step_size * direction
        residual = residual - step_size * along
        if iteration + 1 < ITERS:
            images = image_of(residual)
            norm_next, product = fold_sum(
                (jnp.sum(residual * residual), jnp.sum(residual * images))
            )
            beta_ratio = norm_next / norm_now
            step_size = norm_next / (product - beta_ratio * norm_next / step_size)
            direction = residual + beta_ratio * direction
            along = images + beta_ratio * along
            norm_now = norm_next
    outputs = (solution, residual)
    return outputs


def solution(mesh):
    finer = Mesh(
        mesh.devices.reshape(mesh.shape["groups"], 16, 2, mesh.shape["bin"]),
        ("groups", "seg_0", "seg_1", "bin"),
    )
    in_specs = (
        P(GROUPS_SEG_BIN, None),
        P(("groups", "bin"), None),
        P(GROUPS_SEG, "bin", None, None, None),
        P(GROUPS_SEG, "bin", None, None, None),
        P(GROUPS_SEG, "bin", None, None),
        P(GROUPS_SEG, "bin"),
        P(GROUPS_SEG, "bin", None, None),
        P(GROUPS_SEG, "bin", None, None, None),
        P(GROUPS_SEG, "bin", None, None),
        P(GROUPS_SEG, "bin", None),
        P(GROUPS_SEG, "bin", None, None),
    )
    out_specs = (P(GROUPS_SEG_BIN, None), P(GROUPS_SEG_BIN, None))
    return jax.shard_map(
        shards, mesh=finer, in_specs=in_specs, out_specs=out_specs, check_vma=False
    )
```

profile of v0, /device:TPU:80, one launch (start us, length us, event | category | flops | bytes accessed | tf_op | source)
XLA Modules:
  0.0 300.7 jit_solution(3569220163104865625)
XLA Ops:
  0.6 1.5 broadcast_in_dim.6
  2.2 7.4 %all-to-all-start = ((f32[8,64,128]{2,1,0:T(8,128)}), f32[8,64,128]{2,1,0:T(8,128)S(1)}, u32[]{:S(2)}, u32[]{:S(2)}) async-start(f32[8,64,128]{2,1,0:T(8,128)} %broadcast_in_dim.6), calls=%async_computation | async-start | bytes 524288 | tf_op jit(solution)/shard_map/all_to_all | solution.py:43
  10.2 2.2 collective-permute-start
  13.8 0.8 slice_reduce_fusion
  17.3 0.9 fusion.9
  18.3 1.3 compare_convert_fusion
  20.4 0.7 fusion.72
  22.2 0.9 convolution_multiply_fusion.3
  25.5 0.7 gather_fusion.5
  26.3 5.6 %collective-permute-start.1 = (f32[256,128]{1,0:T(8,128)S(1)}, f32[256,128]{1,0:T(8,128)S(1)}, u32[]{:S(2)}, u32[]{:S(2)}) collective-permute-start(f32[256,128]{1,0:T(8,128)S(1)} %broadcast_multiply_fusion.2), channel_id=1, source_target_pairs={{0,8},{8,16},{16,24},{24,32},{32,40},{40,48},{48,56},{56,64},{64,7... | collective-permute-start | bytes 393224 | tf_op jit(solution)/shard_map/ppermute | solution.py:21
  32.6 0.9 convolution_add_fusion.2
  35.3 0.7 gather_fusion.4
  37.4 1.3 collective-permute-start.2
  39.1 2.0 scatter_fusion
  41.2 2.0 scatter_fusion.1
  43.3 17.7 %all_to_all.30 = f32[8,64,128]{2,1,0:T(8,128)S(1)} all-to-all(f32[8,64,128]{2,1,0:T(8,128)S(1)} %bitcast.164), channel_id=1, replica_groups=mesh['groups'=2,'seg_0'=16,'seg_1'=2,'bin'=8] {'bin'}, dimensions={0} | all-to-all | bytes 524288 | tf_op jit(solution)/shard_map/all_to_all | solution.py:31
  61.0 0.7 copy-done.5
  61.8 13.7 %all_to_all.31 = f32[8,64,128]{2,1,0:T(8,128)S(1)} all-to-all(f32[8,64,128]{2,1,0:T(8,128)S(1)} %broadcast_in_dim.7), channel_id=1, replica_groups=mesh['groups'=2,'seg_0'=16,'seg_1'=2,'bin'=8] {'bin'}, dimensions={0} | all-to-all | bytes 524288 | tf_op jit(solution)/shard_map/all_to_all | solution.py:43
  75.5 0.7 gather_fusion.10
  76.2 0.7 gather_fusion.9
  78.3 0.7 gather_fusion.6
  80.5 4.0 %collective-permute-start.3 = (f32[256,128]{1,0:T(8,128)S(1)}, f32[256,128]{1,0:T(8,128)S(1)}, u32[]{:S(2)}, u32[]{:S(2)}) collective-permute-start(f32[256,128]{1,0:T(8,128)S(1)} %broadcast_multiply_fusion.1), channel_id=1, source_target_pairs={{0,8},{8,16},{16,24},{24,32},{32,40},{40,48},{48,56},{56,64},{64,7... | collective-permute-start | bytes 393224 | tf_op jit(solution)/shard_map/ppermute | solution.py:21
  84.5 0.9 convolution_multiply_fusion.2
  86.8 0.9 convolution_add_fusion.1
  89.0 1.3 collective-permute-start.4
  90.7 2.0 scatter_fusion.2
  92.8 2.2 collective-permute-done.4
  95.0 2.0 scatter_fusion.3
  97.0 13.9 %all_to_all.32 = f32[8,64,128]{2,1,0:T(8,128)S(1)} all-to-all(f32[8,64,128]{2,1,0:T(8,128)S(1)} %bitcast.163), channel_id=1, replica_groups=mesh['groups'=2,'seg_0'=16,'seg_1'=2,'bin'=8] {'bin'}, dimensions={0} | all-to-all | bytes 524288 | tf_op jit(solution)/shard_map/all_to_all | solution.py:31
  111.5 68.4 %all-reduce.1 = (f32[]{:T(128)}, f32[]{:T(128)}) all-reduce(f32[]{:T(128)} %get-tuple-element.9, f32[]{:T(128)} %get-tuple-element.8), channel_id=1, replica_groups=mesh['groups'=2,'seg_0'=16,'seg_1'=2,'bin'=8] {'seg_0'}, use_global_device_ids=true, to_apply=%region_8.0 | all-reduce | flops 2 | bytes 16 | tf_op jit(solution)/shard_map/psum | solution.py:52
  179.9 3.1 %all-reduce.5 = (f32[]{:T(128)}, f32[]{:T(128)}) all-reduce(f32[]{:T(128)} %get-tuple-element.16, f32[]{:T(128)} %get-tuple-element.17), channel_id=1, replica_groups=mesh['groups'=2,'seg_0'=16,'seg_1'=2,'bin'=8] {'seg_1'}, use_global_device_ids=true, to_apply=%region_9.0 | all-reduce | flops 2 | bytes 16 | tf_op jit(solution)/shard_map/psum | solution.py:52
  183.0 15.5 %all-reduce.3 = (f32[]{:T(128)}, f32[]{:T(128)}) all-reduce(f32[]{:T(128)} %get-tuple-element.24, f32[]{:T(128)} %get-tuple-element.25), channel_id=1, replica_groups=mesh['groups'=2,'seg_0'=16,'seg_1'=2,'bin'=8] {'bin'}, use_global_device_ids=true, to_apply=%region_10.0 | all-reduce | flops 2 | bytes 16 | tf_op jit(solution)/shard_map/psum | solution.py:52
  199.9 14.0 %all_to_all.33 = f32[8,64,128]{2,1,0:T(8,128)S(1)} all-to-all(f32[8,64,128]{2,1,0:T(8,128)S(1)} %broadcast_in_dim.8), channel_id=1, replica_groups=mesh['groups'=2,'seg_0'=16,'seg_1'=2,'bin'=8] {'bin'}, dimensions={0} | all-to-all | bytes 524288 | tf_op jit(solution)/shard_map/all_to_all | solution.py:43
  213.9 0.7 gather_fusion.15
  214.7 0.7 gather_fusion.14
  216.1 0.7 gather_fusion.13
  216.8 0.7 gather_fusion.11
  218.3 1.5 collective-permute-start.5
  219.8 0.9 convolution_multiply_fusion.1
  221.8 0.9 convolution_add_fusion
  224.0 1.3 collective-permute-start.6
  225.7 2.0 scatter_fusion.4
  227.8 1.3 collective-permute-done.6
  229.1 2.0 scatter_fusion.5
  231.1 13.3 %all_to_all.34 = f32[8,64,128]{2,1,0:T(8,128)S(1)} all-to-all(f32[8,64,128]{2,1,0:T(8,128)S(1)} %bitcast.160), channel_id=1, replica_groups=mesh['groups'=2,'seg_0'=16,'seg_1'=2,'bin'=8] {'bin'}, dimensions={0} | all-to-all | bytes 524288 | tf_op jit(solution)/shard_map/all_to_all | solution.py:31
  245.1 31.9 %all-reduce = (f32[]{:T(128)}, f32[]{:T(128)}) all-reduce(f32[]{:T(128)} %get-tuple-element.7, f32[]{:T(128)} %get-tuple-element.6), channel_id=1, replica_groups=mesh['groups'=2,'seg_0'=16,'seg_1'=2,'bin'=8] {'seg_0'}, use_global_device_ids=true, to_apply=%region_19.0 | all-reduce | flops 2 | bytes 16 | tf_op jit(solution)/shard_map/psum | solution.py:52
  277.0 3.1 %all-reduce.4 = (f32[]{:T(128)}, f32[]{:T(128)}) all-reduce(f32[]{:T(128)} %get-tuple-element.14, f32[]{:T(128)} %get-tuple-element.15), channel_id=1, replica_groups=mesh['groups'=2,'seg_0'=16,'seg_1'=2,'bin'=8] {'seg_1'}, use_global_device_ids=true, to_apply=%region_20.0 | all-reduce | flops 2 | bytes 16 | tf_op jit(solution)/shard_map/psum | solution.py:52
  280.2 15.4 %all-reduce.2 = (f32[]{:T(128)}, f32[]{:T(128)}) all-reduce(f32[]{:T(128)} %get-tuple-element.22, f32[]{:T(128)} %get-tuple-element.23), channel_id=1, replica_groups=mesh['groups'=2,'seg_0'=16,'seg_1'=2,'bin'=8] {'bin'}, use_global_device_ids=true, to_apply=%region_21.0 | all-reduce | flops 2 | bytes 16 | tf_op jit(solution)/shard_map/psum | solution.py:52
  (127 shorter events, 24.2 us)
Async XLA Ops:
  0.6 15.3 %copy-start = (bf16[1024,128]{1,0:T(8,128)(2,1)S(1)}, bf16[1024,128]{1,0:T(8,128)(2,1)}, u32[]{:S(2)}) copy-start(bf16[1024,128]{1,0:T(8,128)(2,1)} %param.12) | copy-start | bytes 786436
  2.2 7.5 %copy-start.30 = (s32[1,1,2]{2,1,0:T(1,128)S(1)}, s32[1,1,2]{2,1,0:T(1,128)}, u32[]{:S(2)}) copy-start(s32[1,1,2]{2,1,0:T(1,128)} %param.20) | copy-start | bytes 28
  2.2 19.4 %all-to-all-start = ((f32[8,64,128]{2,1,0:T(8,128)}), f32[8,64,128]{2,1,0:T(8,128)S(1)}, u32[]{:S(2)}, u32[]{:S(2)}) async-start(f32[8,64,128]{2,1,0:T(8,128)} %broadcast_in_dim.6), calls=%async_computation | async-start | bytes 524288 | tf_op jit(solution)/shard_map/all_to_all | solution.py:43
  10.2 2.2 copy-start.31
  10.2 9.5 %collective-permute-start = (s32[1]{0:T(128)}, s32[1]{0:T(128)}, u32[]{:S(2)}, u32[]{:S(2)}) collective-permute-start(s32[1]{0:T(128)} %bitcast.23), channel_id=1, source_target_pairs={{0,8},{8,16},{16,24},{24,32},{32,40},{40,48},{48,56},{56,64},{64,7... | collective-permute-start | bytes 20 | tf_op jit(solution)/shard_map/ppermute | solution.py:21
  12.4 4.9 %copy-start.12 = (s32[12]{0:T(128)}, s32[12]{0:T(128)S(1)}, u32[]{:S(2)}) copy-start(s32[12]{0:T(128)S(1)} %get-tuple-element.30) | copy-start | bytes 148
  13.1 9.1 %copy-start.20 = (f32[12]{0:T(128)}, f32[12]{0:T(128)S(1)}, u32[]{:S(2)}) copy-start(f32[12]{0:T(128)S(1)} %compare_convert_fusion.3) | copy-start | bytes 148
  13.1 0.7 copy-start.28
  14.6 0.7 copy-start.29
  15.3 10.2 %copy-start.15 = (s32[1024]{0:T(1024)}, s32[1024]{0:T(1024)S(1)}, u32[]{:S(2)}) copy-start(s32[1024]{0:T(1024)S(1)} %pad_clamp_fusion) | copy-start | bytes 12292
  15.9 5.6 %copy-start.25 = (s32[1024]{0:T(1024)}, s32[1024]{0:T(1024)S(1)}, u32[]{:S(2)}) copy-start(s32[1024]{0:T(1024)S(1)} %get-tuple-element.37) | copy-start | bytes 12292
  15.9 1.0 copy-start.3
  15.9 1.1 copy-start.4
  18.2 1.4 copy-start.2
  18.2 2.1 copy-start.1
  18.3 5.3 %copy-start.27 = (s32[1024]{0:T(1024)}, s32[1024]{0:T(1024)S(1)}, u32[]{:S(2)}) copy-start(s32[1024]{0:T(1024)S(1)} %get-tuple-element.36) | copy-start | bytes 12292
  18.3 5.9 %copy-start.26 = (s32[1024]{0:T(1024)}, s32[1024]{0:T(1024)S(1)}, u32[]{:S(2)}) copy-start(s32[1024]{0:T(1024)S(1)} %get-tuple-element.35) | copy-start | bytes 12292
  19.7 5.1 %copy-start.8 = (f32[2,128]{1,0:T(2,128)}, f32[2,128]{1,0:T(2,128)S(1)}, u32[]{:S(2)}) copy-start(f32[2,128]{1,0:T(2,128)S(1)} %get-tuple-element.5) | copy-start | bytes 3076
  19.7 5.3 %copy-start.10 = (f32[2,128]{1,0:T(2,128)}, f32[2,128]{1,0:T(2,128)S(1)}, u32[]{:S(2)}) copy-start(f32[2,128]{1,0:T(2,128)S(1)} %get-tuple-element.4) | copy-start | bytes 3076
  25.5 0.7 copy-start.18
  26.3 5.6 %copy-start.22 = (s32[2]{0:T(128)S(1)}, s32[2]{0:T(128)}, u32[]{:S(2)}) copy-start(s32[2]{0:T(128)} %get-tuple-element.13) | copy-start | bytes 28
  26.3 9.7 %collective-permute-start.1 = (f32[256,128]{1,0:T(8,128)S(1)}, f32[256,128]{1,0:T(8,128)S(1)}, u32[]{:S(2)}, u32[]{:S(2)}) collective-permute-start(f32[256,128]{1,0:T(8,128)S(1)} %broadcast_multiply_fusion.2), channel_id=1, source_target_pairs={{0,8},{8,16},{16,24},{24,32},{32,40},{40,48},{48,56},{56,64},{64,7... | collective-permute-start | bytes 393224 | tf_op jit(solution)/shard_map/ppermute | solution.py:21
  31.9 0.7 copy-start.13
  33.5 0.6 copy-start.24
  34.6 0.7 copy-start.17
  36.0 0.6 copy-start.7
  37.4 1.3 copy-start.6
  37.4 3.8 %collective-permute-start.2 = (f32[256,128]{1,0:T(8,128)S(1)}, f32[256,128]{1,0:T(8,128)S(1)}, u32[]{:S(2)}, u32[]{:S(2)}) collective-permute-start(f32[256,128]{1,0:T(8,128)S(1)} %multiply_subtract_fusion.2), channel_id=1, source_target_pairs={{8,0},{16,8},{24,16},{32,24},{40,32},{48,40},{56,48},{64,56},{72,6... | collective-permute-start | bytes 393224 | tf_op jit(solution)/shard_map/ppermute | solution.py:21
  61.0 0.8 copy-start.5
  61.8 13.7 %copy-start.16 = (s32[1024]{0:T(1024)S(1)}, s32[1024]{0:T(1024)}, u32[]{:S(2)}) copy-start(s32[1024]{0:T(1024)} %copy-done.15) | copy-start | bytes 12292
  78.3 0.7 copy-start.11
  79.1 0.7 copy-start.9
  79.7 0.7 copy-start.19
  80.4 4.1 %copy-start.21 = (f32[12]{0:T(128)S(1)}, f32[12]{0:T(128)}, u32[]{:S(2)}) copy-start(f32[12]{0:T(128)} %copy-done.20) | copy-start | bytes 148
  80.5 7.8 %collective-permute-start.3 = (f32[256,128]{1,0:T(8,128)S(1)}, f32[256,128]{1,0:T(8,128)S(1)}, u32[]{:S(2)}, u32[]{:S(2)}) collective-permute-start(f32[256,128]{1,0:T(8,128)S(1)} %broadcast_multiply_fusion.1), channel_id=1, source_target_pairs={{0,8},{8,16},{16,24},{24,32},{32,40},{40,48},{48,56},{56,64},{64,7... | collective-permute-start | bytes 393224 | tf_op jit(solution)/shard_map/ppermute | solution.py:21
  85.5 0.7 copy-start.23
  86.1 0.7 copy-start.14
  89.0 6.0 %collective-permute-start.4 = (f32[256,128]{1,0:T(8,128)S(1)}, f32[256,128]{1,0:T(8,128)S(1)}, u32[]{:S(2)}, u32[]{:S(2)}) collective-permute-start(f32[256,128]{1,0:T(8,128)S(1)} %multiply_subtract_fusion.1), channel_id=1, source_target_pairs={{8,0},{16,8},{24,16},{32,24},{40,32},{48,40},{56,48},{64,56},{72,6... | collective-permute-start | bytes 393224 | tf_op jit(solution)/shard_map/ppermute | solution.py:21
  218.3 5.0 %collective-permute-start.5 = (f32[256,128]{1,0:T(8,128)S(1)}, f32[256,128]{1,0:T(8,128)S(1)}, u32[]{:S(2)}, u32[]{:S(2)}) collective-permute-start(f32[256,128]{1,0:T(8,128)S(1)} %broadcast_multiply_fusion), channel_id=1, source_target_pairs={{0,8},{8,16},{16,24},{24,32},{32,40},{40,48},{48,56},{56,64},{64,7... | collective-permute-start | bytes 393224 | tf_op jit(solution)/shard_map/ppermute | solution.py:21
  224.0 5.1 %collective-permute-start.6 = (f32[256,128]{1,0:T(8,128)S(1)}, f32[256,128]{1,0:T(8,128)S(1)}, u32[]{:S(2)}, u32[]{:S(2)}) collective-permute-start(f32[256,128]{1,0:T(8,128)S(1)} %multiply_subtract_fusion), channel_id=1, source_target_pairs={{8,0},{16,8},{24,16},{32,24},{40,32},{48,40},{56,48},{64,56},{72,6... | collective-permute-start | bytes 393224 | tf_op jit(solution)/shard_map/ppermute | solution.py:21
where the time goes:
time: 302 us; the launch traced here: 301 us
  blocking collectives  210 us (70%)
  starting transfers between devices  24.7 us (8%)
  other arithmetic  19.4 us (6%)
  local copies, waits for them, and re-layouts  18.1 us (6%)
  matrix products  16.6 us (5%)
  between operations  7.96 us (3%)
  waiting for transfers between devices  3.95 us (1%)
    psum x6, blocking collectives, one_axis_at_a_time(): x = lax.psum(x, axis)  137 us
    all_to_all x3, blocking collectives, sent_and_summed(): blocks = lax.all_to_all(cut_along(x, dim, devices), axis, 0, 0, tiled=True)  44.9 us
    all_to_all x2, blocking collectives, sent_to_all(): lax.all_to_all(jnp.broadcast_to(x[None], (devices, *x.shape)), axis, 0, 0...  27.7 us
    ppermute x7, starting transfers between devices, from_behind(): return lax.ppermute(x, axis, pairs)  17.2 us
    scatter-add x6, other arithmetic, apply_local(): return summed.at[rows_low].add(own_term).at[rows_up].add(returned)  12.3 us
    all_to_all x1, starting transfers between devices, sent_to_all(): lax.all_to_all(jnp.broadcast_to(x[None], (devices, *x.shape)), axis, 0, 0...  7.45 us
  transfers between devices with their start and end apart: 8, of which 3 were waited for; matrix products, arithmetic and copies ran while one was open for 8% of the time, Pallas kernels for 0%

commit v1 on v0

v1 whole, which is shorter than its diff:
```python
import functools

import jax
import jax.numpy as jnp
from jax import lax
from jax.experimental import pallas as pl
from jax.experimental.pallas import tpu as pltpu
from jax.sharding import PartitionSpec as P

RIDGE = 0.5
APPLIES = 3
MESH = pl.DeviceIdType.MESH
f32 = jnp.float32
bf16 = jnp.bfloat16


def split(x):
    hi = x.astype(bf16)
    return hi, (x - hi.astype(f32)).astype(bf16)


def dot_nn(a, b):
    return jnp.dot(a, b, preferred_element_type=f32)


def dot_nt(a, b):
    return lax.dot_general(a, b, (((1,), (1,)), ((), ())), preferred_element_type=f32)


def kernel(
    n_bin,
    n_seg,
    x0_hbm,
    bins_hbm,
    speed_hbm,
    weight_hbm,
    cells_hbm,
    count_hbm,
    pairs_hbm,
    inner_hbm,
    rows_hbm,
    face_hbm,
    sol_ref,
    res_ref,
    field,
    below,
    above,
    part,
    landed,
    bins,
    speed,
    weight,
    cells,
    count,
    pairs,
    hits,
    inner,
    rows,
    rows_below,
    rows_above,
    face,
    face_above,
    gain,
    v_wide,
    v_tall,
    pulled,
    w_hi,
    w_lo,
    f_below,
    f_above,
    degree,
    rhs,
    wide,
    sums_mine,
    sums_seg,
    sums_far,
    sums_bin,
    load_sem,
    gather_send,
    gather_recv,
    below_send,
    below_recv,
    above_send,
    above_recv,
    scatter_send,
    scatter_recv,
    setup_send,
    setup_recv,
    sums_send,
    sums_recv,
):
    seg = lax.axis_index("seg")
    bin_ = lax.axis_index("bin")
    own = x0_hbm.shape[0]
    width = x0_hbm.shape[1]
    n_tiles = speed.shape[0]
    tile = speed.shape[1]
    n_inner = inner.shape[0]
    part_rows = own * n_bin
    n_blocks = part_rows // tile
    half = n_seg // 4
    seg_next = lax.rem(seg + 1, n_seg)
    seg_prev = lax.rem(seg + n_seg - 1, n_seg)

    def seg_at(offset):
        return lax.rem(seg + (offset + n_seg), n_seg)

    def bin_at(offset):
        return lax.rem(bin_ + offset, n_bin)

    def own_slice():
        return pl.ds(pl.multiple_of(bin_ * own, own), own)

    loads = []
    for at, (src, dst) in enumerate(
        (
            (x0_hbm, field.at[0, own_slice()]),
            (rows_hbm, rows),
            (cells_hbm, cells),
            (count_hbm, count),
            (pairs_hbm, pairs),
            (face_hbm, face),
            (bins_hbm, bins),
            (weight_hbm, weight),
            (speed_hbm, speed),
            (inner_hbm, inner),
        )
    ):
        copy = pltpu.make_async_copy(src, dst, load_sem.at[at])
        copy.start()
        loads.append(copy)

    barrier = pltpu.get_barrier_semaphore()
    seg_offsets = [d for d in range(-half, half + 1) if d != 0]
    for d in range(1, n_bin):
        pl.semaphore_signal(barrier, inc=1, device_id={"bin": bin_at(d)}, device_id_type=MESH)
    for d in seg_offsets:
        pl.semaphore_signal(barrier, inc=1, device_id={"seg": seg_at(d)}, device_id_type=MESH)

    def slots_and_gain():
        for load in loads[2:5] + loads[6:8]:
            load.wait()
        targets = [cells[k, 0] for k in range(n_tiles)]
        targets += [pairs[j // 2, j % 2] for j in range(2 * n_inner)]
        for item, target in enumerate(targets):
            for b in range(n_blocks):
                away = target - b
                hits[item, b] = (1 - jnp.minimum(away * away, 1)).astype(f32)
        for k in range(n_tiles):
            live = jnp.clip(count[0, 0] - k, 0, 1).astype(f32)
            gain[k] = weight[k].astype(f32) * live
            chosen = bins[cells[k, 1]]
            v_wide[k, :, :width] = chosen
            v_wide[k, :, width:] = chosen
            v_tall[k, :tile] = chosen
            v_tall[k, tile:] = chosen

    def add_up(items, block):
        total = None
        for ref_at, item in items:
            term = ref_at() * hits[item, block]
            total = term if total is None else total + term
        return total

    def right_side():
        loads[8].wait()
        for k in range(n_tiles):
            weighted = (weight[k].astype(f32) * speed[k].astype(f32)).astype(bf16)
            live = jnp.clip(count[0, 0] - k, 0, 1).astype(f32)
            pulled[k] = dot_nn(weighted, v_tall[k, :tile]) * live
        for b in range(n_blocks):
            items = [((lambda k=k: pulled[k]), k) for k in range(n_tiles)]
            rhs[b * tile : (b + 1) * tile] = add_up(items, b)

    def inner_setup():
        loads[9].wait()
        for j in range(n_inner):
            forward = inner[j]
            hi, lo = split(forward)
            w_hi[2 * j] = hi
            w_lo[2 * j] = lo
            back = forward.T
            hi, lo = split(back)
            w_hi[2 * j + 1] = hi
            w_lo[2 * j + 1] = lo
            pulled[2 * j] = jnp.broadcast_to(forward.sum(1, keepdims=True), (tile, width))
            pulled[2 * j + 1] = jnp.broadcast_to(back.sum(1, keepdims=True), (tile, width))

    def inner_degree(b):
        items = [((lambda j=j: pulled[j]), n_tiles + j) for j in range(2 * n_inner)]
        return add_up(items, b)

    def one_hot(row_ref, which):
        n_face = row_ref.shape[1]
        listed = jnp.broadcast_to(row_ref[which : which + 1, :], (part_rows, n_face))
        at = lax.broadcasted_iota(jnp.int32, (part_rows, n_face), 0)
        return jnp.where(listed == at, 1.0, 0.0).astype(bf16)

    def face_setup():
        low_own = one_hot(rows, 0)
        up_own = one_hot(rows, 1)
        up_below = one_hot(rows_below, 1)
        low_above = one_hot(rows_above, 0)
        down = jnp.where(seg > 0, 1.0, 0.0).astype(f32)
        up = jnp.where(seg < n_seg - 1, 1.0, 0.0).astype(f32)
        mine = split(face[...] * down)
        theirs = split(face_above[...] * up)
        degrees = jnp.zeros((part_rows, 1), f32)
        for p in range(2):
            picked = dot_nn(low_own, mine[p]).astype(bf16)
            whole = dot_nt(picked, up_below)
            f_below[p] = whole.astype(bf16)
            degrees = degrees + whole.sum(1, keepdims=True)
            picked = dot_nt(up_own, theirs[p]).astype(bf16)
            whole = dot_nt(picked, low_above)
            f_above[p] = whole.astype(bf16)
            degrees = degrees + whole.sum(1, keepdims=True)
        degree[...] = jnp.broadcast_to(degrees, (part_rows, width))
        for b in range(n_blocks):
            degree[b * tile : (b + 1) * tile] += inner_degree(b)

    def doubled(product):
        return product[:, :width] + product[:, width:]

    def local_terms(step):
        hi, lo = split(field[step])
        for b in range(n_blocks):
            wide[b, :, :width] = hi[b * tile : (b + 1) * tile]
            wide[b, :, width:] = lo[b * tile : (b + 1) * tile]
        for k in range(n_tiles):
            picked = wide[cells[k, 0]]
            scores = dot_nt(picked, v_wide[k]) * gain[k]
            hi, lo = split(scores)
            pulled[k] = dot_nn(jnp.concatenate([hi, lo], axis=1), v_tall[k])
        for j in range(n_inner):
            for way in range(2):
                picked = wide[pairs[j, 1 - way]]
                product = doubled(dot_nn(w_hi[2 * j + way], picked))
                product = product + dot_nn(w_lo[2 * j + way], picked[:, :width])
                pulled[n_tiles + 2 * j + way] = -product

    def face_terms(step):
        total = None
        for matrix, source in ((f_below, below), (f_above, above)):
            hi, lo = split(source[step])
            both = jnp.concatenate([hi, lo], axis=1)
            product = doubled(dot_nn(matrix[0], both)) + dot_nn(matrix[1], hi)
            total = product if total is None else total + product
        return total

    def join(step, faces):
        items = [((lambda k=k: pulled[k]), k) for k in range(n_tiles)]
        for j in range(2 * n_inner):
            items.append(((lambda j=j: pulled[n_tiles + j]), n_tiles + j))
        for b in range(n_blocks):
            at = slice(b * tile, (b + 1) * tile)
            value = add_up(items, b) + degree[at] * field[step, at] - faces[at]
            part[step, at] = rhs[at] - value if step == 0 else value

    order = sorted(range(1, n_bin), key=lambda d: -min(d, n_bin - d))

    def to_bin(src, dst, send, recv, d):
        return pltpu.make_async_remote_copy(
            src_ref=src, dst_ref=dst, send_sem=send, recv_sem=recv,
            device_id={"bin": bin_at(d)}, device_id_type=MESH,
        )

    def to_seg(src, dst, send, recv, where):
        return pltpu.make_async_remote_copy(
            src_ref=src, dst_ref=dst, send_sem=send, recv_sem=recv,
            device_id={"seg": where}, device_id_type=MESH,
        )

    def forward(step, source):
        rows_at = pl.ds(pl.multiple_of(source * own, own), own)
        block = field.at[step, rows_at]
        to_seg(block, below.at[step, rows_at], below_send.at[step], below_recv.at[step], seg_next).start()
        to_seg(block, above.at[step, rows_at], above_send.at[step], above_recv.at[step], seg_prev).start()

    def gather_start(step):
        mine = field.at[step, own_slice()]
        for d in order:
            to_bin(mine, mine, gather_send.at[step], gather_recv.at[step, d], d).start()
        forward(step, bin_)

    def gather_finish(step):
        for d in reversed(order):
            source = lax.rem(bin_ + (n_bin - d), n_bin)
            rows_at = pl.ds(pl.multiple_of(source * own, own), own)
            block = field.at[step, rows_at]
            pltpu.make_async_copy(block, block, gather_recv.at[step, d]).wait()
            forward(step, source)

    def faces_finish(step):
        pltpu.make_async_copy(below.at[step], below.at[step], below_recv.at[step]).wait()
        pltpu.make_async_copy(above.at[step], above.at[step], above_recv.at[step]).wait()

    def scatter_start(step):
        for d in order:
            target = bin_at(d)
            block = part.at[step, pl.ds(pl.multiple_of(target * own, own), own)]
            to_bin(block, landed.at[step, d - 1], scatter_send.at[step], scatter_recv.at[step], d).start()

    def scatter_finish(step):
        pltpu.make_async_copy(landed.at[step], landed.at[step], scatter_recv.at[step]).wait()
        total = part[step, own_slice()]
        for d in range(n_bin - 1):
            total = total + landed[step, d]
        return total

    window = [e for e in range(-half + 1, half + 1) if e != 0]

    def two_sums(first, second):
        lanes = lax.broadcasted_iota(jnp.int32, (1, width), 1)
        first = first.sum(0, keepdims=True)
        second = second.sum(0, keepdims=True)
        first = first + pltpu.roll(first, width // 2, 1)
        second = second + pltpu.roll(second, width // 2, 1)
        return jnp.where(lanes < width // 2, first, second)

    def sums_start(turn, value):
        sums_mine[turn, 0] = value
        for at, e in enumerate(window):
            to_seg(sums_mine.at[turn, 0], sums_seg.at[turn, at], sums_send.at[turn, 0], sums_recv.at[turn, 0], seg_at(e)).start()

    def sums_second(turn):
        pltpu.make_async_copy(sums_seg.at[turn], sums_seg.at[turn], sums_recv.at[turn, 0]).wait()
        total = sums_mine[turn, 0]
        for at in range(len(window)):
            total = total + sums_seg[turn, at]
        sums_mine[turn, 1] = total
        for at, e in enumerate((-half, half)):
            to_seg(sums_mine.at[turn, 1], sums_far.at[turn, at], sums_send.at[turn, 1], sums_recv.at[turn, 1], seg_at(e)).start()

    def sums_third(turn):
        pltpu.make_async_copy(sums_far.at[turn], sums_far.at[turn], sums_recv.at[turn, 1]).wait()
        total = sums_far[turn, 0] + sums_far[turn, 1]
        sums_mine[turn, 2] = total
        for d in order:
            to_bin(sums_mine.at[turn, 2], sums_bin.at[turn, d - 1], sums_send.at[turn, 2], sums_recv.at[turn, 2], d).start()

    def sums_finish(turn):
        pltpu.make_async_copy(sums_bin.at[turn], sums_bin.at[turn], sums_recv.at[turn, 2]).wait()
        total = sums_mine[turn, 2]
        for d in range(n_bin - 1):
            total = total + sums_bin[turn, d]
        lanes = lax.broadcasted_iota(jnp.int32, (1, width), 1)
        first = jnp.sum(jnp.where(lanes < width // 2, total, 0.0), axis=1, keepdims=True)
        second = jnp.sum(jnp.where(lanes < width // 2, 0.0, total), axis=1, keepdims=True)
        return first, second

    slots_and_gain()
    loads[0].wait()
    loads[1].wait()
    loads[5].wait()
    pl.semaphore_wait(barrier, n_bin - 1 + len(seg_offsets))
    to_seg(rows, rows_below, setup_send.at[0], setup_recv.at[0], seg_next).start()
    to_seg(rows, rows_above, setup_send.at[1], setup_recv.at[1], seg_prev).start()
    gather_start(0)
    to_seg(face, face_above, setup_send.at[2], setup_recv.at[2], seg_prev).start()
    right_side()
    inner_setup()
    gather_finish(0)
    pltpu.make_async_copy(rows, rows_below, setup_recv.at[0]).wait()
    pltpu.make_async_copy(rows, rows_above, setup_recv.at[1]).wait()
    pltpu.make_async_copy(face, face_above, setup_recv.at[2]).wait()
    face_setup()
    local_terms(0)
    faces_finish(0)
    join(0, face_terms(0))
    scatter_start(0)
    start = field[0, own_slice()]
    residual = scatter_finish(0) - RIDGE * start
    field[1, own_slice()] = residual

    gather_start(1)
    gather_finish(1)
    local_terms(1)
    faces_finish(1)
    join(1, face_terms(1))
    square = residual * residual
    sums_start(0, two_sums(square, field[1] * part[1]))
    scatter_start(1)
    sums_second(0)
    image = scatter_finish(1) + RIDGE * field[1, own_slice()]
    field[2, own_slice()] = image
    gather_start(2)
    sums_third(0)

    gather_finish(2)
    local_terms(2)
    faces_finish(2)
    join(2, face_terms(2))
    norm, product = sums_finish(0)
    product = product + RIDGE * norm
    step_one = norm / product
    residual = field[1, own_slice()]
    image = field[2, own_slice()]
    later = residual - step_one * image
    whole = field[1] - step_one * field[2]
    whole_image = part[1] - step_one * part[2]
    sums_start(1, two_sums(later * later, whole * whole_image))
    scatter_start(2)
    sums_second(1)
    sums_third(1)
    image_two = scatter_finish(2) + RIDGE * field[2, own_slice()]
    norm_next, product_next = sums_finish(1)
    product_next = product_next + RIDGE * norm_next
    beta = norm_next / norm
    step_two = norm_next / (product_next - beta * norm_next / step_one)
    residual = field[1, own_slice()]
    image = field[2, own_slice()]
    later = residual - step_one * image
    later_image = image - step_one * image_two
    direction = later + beta * residual
    along = later_image + beta * image
    sol_ref[...] = field[0, own_slice()] + step_one * residual + step_two * direction
    res_ref[...] = later - step_two * along

    pltpu.make_async_copy(rows, rows, setup_send.at[0]).wait()
    pltpu.make_async_copy(rows, rows, setup_send.at[1]).wait()
    pltpu.make_async_copy(face, face, setup_send.at[2]).wait()
    for step in range(APPLIES):
        pltpu.make_async_copy(landed.at[step], landed.at[step], gather_send.at[step]).wait()
        pltpu.make_async_copy(landed.at[step], landed.at[step], scatter_send.at[step]).wait()
        pltpu.make_async_copy(below.at[step], below.at[step], below_send.at[step]).wait()
        pltpu.make_async_copy(above.at[step], above.at[step], above_send.at[step]).wait()
    for turn in range(2):
        pltpu.make_async_copy(sums_seg.at[turn], sums_seg.at[turn], sums_send.at[turn, 0]).wait()
        pltpu.make_async_copy(sums_far.at[turn], sums_far.at[turn], sums_send.at[turn, 1]).wait()
        pltpu.make_async_copy(sums_bin.at[turn], sums_bin.at[turn], sums_send.at[turn, 2]).wait()


def shards(
    n_bin,
    n_seg,
    start_factors,
    bin_factors,
    tile_speed,
    tile_weight,
    tile_cells,
    tile_count,
    inner_pairs,
    inner_weight,
    face_rows,
    face_count,
    face_weight,
):
    own, width = start_factors.shape
    n_tiles, tile = tile_speed.shape[2:4]
    n_inner = inner_weight.shape[2]
    n_face = face_rows.shape[3]
    part_rows = own * n_bin
    slots = jnp.arange(n_face, dtype=jnp.int32)
    listed = jnp.where(slots[None, :] < face_count[0, 0][:, None], face_rows[0, 0], -1)
    half = n_seg // 4
    window = 2 * half - 1
    any_ = pl.BlockSpec(memory_space=pl.ANY)
    vmem = pl.BlockSpec(memory_space=pltpu.VMEM)
    dma = pltpu.SemaphoreType.DMA
    out = jax.ShapeDtypeStruct((own, width), f32)
    call = pl.pallas_call(
        functools.partial(kernel, n_bin, n_seg),
        out_shape=(out, out),
        in_specs=[any_] * 10,
        out_specs=(vmem, vmem),
        scratch_shapes=[
            pltpu.VMEM((APPLIES, part_rows, width), f32),
            pltpu.VMEM((APPLIES, part_rows, width), f32),
            pltpu.VMEM((APPLIES, part_rows, width), f32),
            pltpu.VMEM((APPLIES, part_rows, width), f32),
            pltpu.VMEM((APPLIES, n_bin - 1, own, width), f32),
            pltpu.VMEM((bin_factors.shape[0] // tile, tile, width), bf16),
            pltpu.VMEM((n_tiles, tile, tile), bf16),
            pltpu.VMEM((n_tiles, tile, tile), bf16),
            pltpu.SMEM((n_tiles, 2), jnp.int32),
            pltpu.SMEM((1, 1), jnp.int32),
            pltpu.SMEM((n_inner, 2), jnp.int32),
            pltpu.SMEM((n_tiles + 2 * n_inner, part_rows // tile), f32),
            pltpu.VMEM((n_inner, tile, tile), f32),
            pltpu.VMEM((2, n_face), jnp.int32),
            pltpu.VMEM((2, n_face), jnp.int32),
            pltpu.VMEM((2, n_face), jnp.int32),
            pltpu.VMEM((n_face, n_face), f32),
            pltpu.VMEM((n_face, n_face), f32),
            pltpu.VMEM((n_tiles, tile, tile), f32),
            pltpu.VMEM((n_tiles, tile, 2 * width), bf16),
            pltpu.VMEM((n_tiles, 2 * tile, width), bf16),
            pltpu.VMEM((n_tiles + 2 * n_inner, tile, width), f32),
            pltpu.VMEM((2 * n_inner, tile, tile), bf16),
            pltpu.VMEM((2 * n_inner, tile, tile), bf16),
            pltpu.VMEM((2, part_rows, part_rows), bf16),
            pltpu.VMEM((2, part_rows, part_rows), bf16),
            pltpu.VMEM((part_rows, width), f32),
            pltpu.VMEM((part_rows, width), f32),
            pltpu.VMEM((part_rows // tile, tile, 2 * width), bf16),
            pltpu.VMEM((2, 3, 1, width), f32),
            pltpu.VMEM((2, window, 1, width), f32),
            pltpu.VMEM((2, 2, 1, width), f32),
            pltpu.VMEM((2, n_bin - 1, 1, width), f32),
            dma((10,)),
            dma((APPLIES,)),
            dma((APPLIES, n_bin)),
            dma((APPLIES,)),
            dma((APPLIES,)),
            dma((APPLIES,)),
            dma((APPLIES,)),
            dma((APPLIES,)),
            dma((APPLIES,)),
            dma((3,)),
            dma((3,)),
            dma((2, 3)),
            dma((2, 3)),
        ],
        compiler_params=pltpu.CompilerParams(collective_id=0, has_side_effects=True),
    )
    return call(
        start_factors,
        bin_factors.reshape(-1, tile, width),
        tile_speed[0, 0],
        tile_weight[0, 0],
        tile_cells[0, 0],
        tile_count,
        inner_pairs[0, 0],
        inner_weight[0, 0],
        listed,
        face_weight[0, 0],
    )


def solution(mesh):
    lead = ("groups", "seg")
    rows = P(("groups", "seg", "bin"), None)
    in_specs = (
        rows,
        P(("groups", "bin"), None),
        P(lead, "bin", None, None, None),
        P(lead, "bin", None, None, None),
        P(lead, "bin", None, None),
        P(lead, "bin"),
        P(lead, "bin", None, None),
        P(lead, "bin", None, None, None),
        P(lead, "bin", None, None),
        P(lead, "bin", None),
        P(lead, "bin", None, None),
    )
    body = functools.partial(shards, mesh.shape["bin"], mesh.shape["seg"])
    return jax.shard_map(
        body, mesh=mesh, in_specs=in_specs, out_specs=(rows, rows), check_vma=False
    )
```

time: 302 us -> 123 us (0.41)
  blocking collectives: 210 us -> 0 us
  Pallas kernels: 0 us -> 117 us
  starting transfers between devices: 24.7 us -> 0 us
  other arithmetic: 19.4 us -> 0.65 us
  matrix products: 16.6 us -> 0 us
  local copies, waits for them, and re-layouts: 18.1 us -> 3.38 us
  between operations: 7.96 us -> 1.31 us
  waiting for transfers between devices: 3.95 us -> 0 us
    psum x6 -> x0, blocking collectives: 137 us -> none  [one_axis_at_a_time(): x = lax.psum(x, axis)]
    pallas_call x0 -> x1, Pallas kernels: none -> 117 us  [shards(): call(start_factors, bin_factors.reshape(-1, tile, width), tile_speed[0, 0...]
    all_to_all x5 -> x0, blocking collectives: 72.6 us -> none  [the longest x3 44.9 us: sent_and_summed(): blocks = lax.all_to_all(cut_along(x, dim, devices), axis, 0, 0, tiled=True)]
    ppermute x7 -> x0, starting transfers between devices: 17.2 us -> none  [from_behind(): return lax.ppermute(x, axis, pairs)]
    dot_general x29 -> x0, matrix products: 16.6 us -> none  [the longest x3 2.81 us: apply_local(): jnp.einsum('kir,kjr->kij', picked, bins_wide, precision=highest) * tile_gain]
    scatter-add x6 -> x0, other arithmetic: 12.3 us -> none  [apply_local(): return summed.at[rows_low].add(own_term).at[rows_up].add(returned)]
    gather x16 -> x0, local copies, waits for them, and re-layouts: 10.9 us -> none  [the longest x3 2.19 us: apply_local(): upper_face = whole_rows[rows_up] * mask_up[:, None]]
    all_to_all x1 -> x0, starting transfers between devices: 7.45 us -> none  [sent_to_all(): lax.all_to_all(jnp.broadcast_to(x[None], (devices, *x.shape)), axis, 0, 0...]
  transfers between devices with their start and end apart: 8 -> 0, of which waited for: 3 -> 0; matrix products, arithmetic and copies ran while one was open for 8% -> 0% of each run, Pallas kernels for 0% -> 0%
where the time goes in v1:
time: 123 us
  Pallas kernels  117 us (95%)
  local copies, waits for them, and re-layouts  3.38 us (3%)
  between operations  1.31 us (1%)
    pallas_call x1, Pallas kernels, shards(): call(start_factors, bin_factors.reshape(-1, tile, width), tile_speed[0, 0...  117 us
    unnamed x10, local copies, waits for them, and re-layouts  2.7 us

profile of v1, /device:TPU:80, one launch (start us, length us, event | category | flops | bytes accessed | tf_op | source)
XLA Modules:
  0.0 122.7 jit_solution(8135677566583115267)
XLA Ops:
  1.3 0.0 copy-start.1
  1.3 0.0 copy-start.3
  1.3 0.7 copy-done.1
  2.0 0.0 copy-done.3
  2.0 0.0 copy-start.2
  2.0 0.6 compare_select_fusion.rows_hbm
  2.6 0.0 copy-done.2
  2.6 0.7 copy.13.cells_hbm
  3.3 117.4 %shard_map.122 = (f32[64,128]{1,0:T(8,128)}, f32[64,128]{1,0:T(8,128)}) custom-call(f32[64,128]{1,0:T(8,128)} %x0_hbm.1, bf16[8,128,128]{2,1,0:T(8,128)(2,1)} %bitcast.12, bf16[12,128,128]{2,1,0:T(8,128)(2,1)} %bitcast.10, bf16[12,128,128]{2,1,0:T(8,128)(2,1)} %bitcast.11, s32[12,2]{1,0:T(8,128)} %copy.13.cells_hbm, s32[1,1]{1,0:T(1,128)S(6)} %copy.16.count_hbm, ...), custom_call_target="tpu_custom_call" | custom-call | tf_op jit(solution)/shard_map/pallas_call | solution.py:517
  120.7 0.0 copy-start
  120.7 1.4 %copy.17 = f32[64,128]{1,0:T(8,128)} copy(f32[64,128]{1,0:T(8,128)} %get-tuple-element.4) | data formatting | bytes 65536
  122.1 0.0 copy-done
  122.1 0.6 copy.18
Async XLA Ops:
  1.3 0.7 copy-start.1
  1.3 0.7 copy-start.3
  2.0 0.7 copy-start.2
  120.7 1.4 %copy-start = (f32[64,128]{1,0:T(8,128)S(1)}, f32[64,128]{1,0:T(8,128)}, u32[]{:S(2)}) copy-start(f32[64,128]{1,0:T(8,128)} %get-tuple-element.5) | copy-start | bytes 98308

commit v2 on v1

--- a/solution.py
+++ b/solution.py
@@ -39,14 +39,19 @@
     pairs_hbm,
     inner_hbm,
     rows_hbm,
+    lives_hbm,
     face_hbm,
-    sol_ref,
-    res_ref,
+    step_ref,
+    later_ref,
+    along_ref,
     field,
     below,
     above,
     part,
     landed,
+    halves,
+    fulls,
+    passed,
     bins,
     speed,
     weight,
@@ -55,6 +60,8 @@
     pairs,
     hits,
     inner,
+    lives,
+    listed,
     rows,
     rows_below,
     rows_above,
@@ -111,36 +118,34 @@
     def own_slice():
         return pl.ds(pl.multiple_of(bin_ * own, own), own)
 
-    loads = []
-    for at, (src, dst) in enumerate(
-        (
-            (x0_hbm, field.at[0, own_slice()]),
-            (rows_hbm, rows),
-            (cells_hbm, cells),
-            (count_hbm, count),
-            (pairs_hbm, pairs),
-            (face_hbm, face),
-            (bins_hbm, bins),
-            (weight_hbm, weight),
-            (speed_hbm, speed),
-            (inner_hbm, inner),
-        )
-    ):
-        copy = pltpu.make_async_copy(src, dst, load_sem.at[at])
-        copy.start()
-        loads.append(copy)
-
     barrier = pltpu.get_barrier_semaphore()
     seg_offsets = [d for d in range(-half, half + 1) if d != 0]
+    pairs_of = (
+        (x0_hbm, field.at[0, own_slice()]),
+        (rows_hbm, listed),
+        (lives_hbm, lives),
+        (face_hbm, face),
+        (cells_hbm, cells),
+        (count_hbm, count),
+        (pairs_hbm, pairs),
+        (bins_hbm, bins),
+        (weight_hbm, weight),
+        (speed_hbm, speed),
+        (inner_hbm, inner),
+    )
+    loads = [pltpu.make_async_copy(src, dst, load_sem.at[at]) for at, (src, dst) in enumerate(pairs_of)]
+    loads[0].start()
     for d in range(1, n_bin):
         pl.semaphore_signal(barrier, inc=1, device_id={"bin": bin_at(d)}, device_id_type=MESH)
     for d in seg_offsets:
         pl.semaphore_signal(barrier, inc=1, device_id={"seg": seg_at(d)}, device_id_type=MESH)
+    for load in loads[1:]:
+        load.start()
 
     def slots_and_gain():
-        for load in loads[2:5] + loads[6:8]:
+        for load in loads[4:9]:
             load.wait()
-        targets = [cells[k, 0] for k in range(n_tiles)]
+        targets = [cells[0, k] for k in range(n_tiles)]
         targets += [pairs[j // 2, j % 2] for j in range(2 * n_inner)]
         for item, target in enumerate(targets):
             for b in range(n_blocks):
@@ -149,7 +154,7 @@
         for k in range(n_tiles):
             live = jnp.clip(count[0, 0] - k, 0, 1).astype(f32)
             gain[k] = weight[k].astype(f32) * live
-            chosen = bins[cells[k, 1]]
+            chosen = bins[cells[1, k]]
             v_wide[k, :, :width] = chosen
             v_wide[k, :, width:] = chosen
             v_tall[k, :tile] = chosen
@@ -163,7 +168,7 @@
         return total
 
     def right_side():
-        loads[8].wait()
+        loads[9].wait()
         for k in range(n_tiles):
             weighted = (weight[k].astype(f32) * speed[k].astype(f32)).astype(bf16)
             live = jnp.clip(count[0, 0] - k, 0, 1).astype(f32)
@@ -173,7 +178,7 @@
             rhs[b * tile : (b + 1) * tile] = add_up(items, b)
 
     def inner_setup():
-        loads[9].wait()
+        loads[10].wait()
         for j in range(n_inner):
             forward = inner[j]
             hi, lo = split(forward)
@@ -228,7 +233,7 @@
             wide[b, :, :width] = hi[b * tile : (b + 1) * tile]
             wide[b, :, width:] = lo[b * tile : (b + 1) * tile]
         for k in range(n_tiles):
-            picked = wide[cells[k, 0]]
+            picked = wide[cells[0, k]]
             scores = dot_nt(picked, v_wide[k]) * gain[k]
             hi, lo = split(scores)
             pulled[k] = dot_nn(jnp.concatenate([hi, lo], axis=1), v_tall[k])
@@ -277,35 +282,87 @@
         to_seg(block, below.at[step, rows_at], below_send.at[step], below_recv.at[step], seg_next).start()
         to_seg(block, above.at[step, rows_at], above_send.at[step], above_recv.at[step], seg_prev).start()
 
+    slot_of = {-1: 0, 1: 1, -2: 2, 2: 3, -3: 4, 3: 5, -4: 6, 4: 7}
+
+    def block_rows(offset, part_of=None):
+        at = lax.rem(bin_ + (offset + n_bin), n_bin) * own
+        size = own if part_of is None else own // 2
+        if part_of:
+            at = at + size
+        return pl.ds(pl.multiple_of(at, size), size)
+
+    def gather_send_to(step, source, to, part_of=None):
+        block = field.at[step, block_rows(source, part_of)]
+        recv = gather_recv.at[step, slot_of[source - to]]
+        to_bin(block, block, gather_send.at[step], recv, to + n_bin).start()
+
+    def gather_wait(step, source, part_of=None):
+        block = field.at[step, block_rows(source, part_of)]
+        pltpu.make_async_copy(block, block, gather_recv.at[step, slot_of[source]]).wait()
+        rows_at = block_rows(source, part_of)
+        to_seg(block, below.at[step, rows_at], below_send.at[step], below_recv.at[step], seg_next).start()
+        to_seg(block, above.at[step, rows_at], above_send.at[step], above_recv.at[step], seg_prev).start()
+
     def gather_start(step):
-        mine = field.at[step, own_slice()]
-        for d in order:
-            to_bin(mine, mine, gather_send.at[step], gather_recv.at[step, d], d).start()
+        for to in (2, -2, 1, -1):
+            gather_send_to(step, 0, to)
         forward(step, bin_)
 
+    def gather_relay(step):
+        for side in (-1, 1):
+            source = 2 * side
+            block = field.at[step, block_rows(source)]
+            pltpu.make_async_copy(block, block, gather_recv.at[step, slot_of[source]]).wait()
+            gather_send_to(step, source, -side)
+            gather_send_to(step, source, -2 * side, 0 if side < 0 else 1)
+            forward(step, lax.rem(bin_ + (source + n_bin), n_bin))
+        gather_wait(step, -1)
+        gather_wait(step, 1)
+
     def gather_finish(step):
-        for d in reversed(order):
-            source = lax.rem(bin_ + (n_bin - d), n_bin)
-            rows_at = pl.ds(pl.multiple_of(source * own, own), own)
-            block = field.at[step, rows_at]
-            pltpu.make_async_copy(block, block, gather_recv.at[step, d]).wait()
-            forward(step, source)
+        gather_wait(step, -3)
+        gather_wait(step, 3)
+        gather_wait(step, -4, 0)
+        gather_wait(step, 4, 1)
 
     def faces_finish(step):
         pltpu.make_async_copy(below.at[step], below.at[step], below_recv.at[step]).wait()
         pltpu.make_async_copy(above.at[step], above.at[step], above_recv.at[step]).wait()
 
+    def scatter_send_to(step, src, dst, slot, to):
+        to_bin(src, dst, scatter_send.at[step], scatter_recv.at[step, slot], to + n_bin).start()
+
     def scatter_start(step):
-        for d in order:
-            target = bin_at(d)
-            block = part.at[step, pl.ds(pl.multiple_of(target * own, own), own)]
-            to_bin(block, landed.at[step, d - 1], scatter_send.at[step], scatter_recv.at[step], d).start()
+        for side in (-1, 1):
+            at = 0 if side < 0 else 1
+            scatter_send_to(step, part.at[step, block_rows(4, 1 - at)], halves.at[step, at], at, 2 * side)
+            scatter_send_to(step, part.at[step, block_rows(3 * side)], fulls.at[step, at], 2 + at, side)
+        for side in (-1, 1):
+            at = 0 if side < 0 else 1
+            scatter_send_to(step, part.at[step, block_rows(side)], landed.at[step, at], 4 + at, side)
+
+    def arrived(step, ref, slot):
+        pltpu.make_async_copy(ref, ref, scatter_recv.at[step, slot]).wait()
+
+    def scatter_relay(step):
+        for side in (-1, 1):
+            at = 0 if side < 0 else 1
+            size = own // 2
+            arrived(step, fulls.at[step, at], 2 + at)
+            arrived(step, halves.at[step, at], at)
+            total = part[step, block_rows(2 * side)] + fulls[step, at]
+            other = 1 - at
+            mine = slice(other * size, (other + 1) * size)
+            rest = slice(at * size, (at + 1) * size)
+            passed[step, at, rest] = total[rest]
+            passed[step, at, mine] = total[mine] + halves[step, at]
+            scatter_send_to(step, passed.at[step, at], landed.at[step, 2 + at], 6 + at, 2 * side)
 
     def scatter_finish(step):
-        pltpu.make_async_copy(landed.at[step], landed.at[step], scatter_recv.at[step]).wait()
         total = part[step, own_slice()]
-        for d in range(n_bin - 1):
-            total = total + landed[step, d]
+        for at in range(4):
+            arrived(step, landed.at[step, at], 4 + at)
+            total = total + landed[step, at]
         return total
 
     window = [e for e in range(-half + 1, half + 1) if e != 0]
@@ -349,31 +406,39 @@
         second = jnp.sum(jnp.where(lanes < width // 2, 0.0, total), axis=1, keepdims=True)
         return first, second
 
-    slots_and_gain()
+    for load in loads[1:3]:
+        load.wait()
+    slot_at = lax.broadcasted_iota(jnp.int32, (1, listed.shape[1]), 1)
+    for side in range(2):
+        own_list = listed[side : side + 1, :]
+        rows[side : side + 1, :] = jnp.where(slot_at < lives[0, side], own_list, -1)
     loads[0].wait()
-    loads[1].wait()
-    loads[5].wait()
+    loads[3].wait()
     pl.semaphore_wait(barrier, n_bin - 1 + len(seg_offsets))
+    to_seg(face, face_above, setup_send.at[2], setup_recv.at[2], seg_prev).start()
+    gather_start(0)
     to_seg(rows, rows_below, setup_send.at[0], setup_recv.at[0], seg_next).start()
     to_seg(rows, rows_above, setup_send.at[1], setup_recv.at[1], seg_prev).start()
-    gather_start(0)
-    to_seg(face, face_above, setup_send.at[2], setup_recv.at[2], seg_prev).start()
+    slots_and_gain()
     right_side()
+    gather_relay(0)
     inner_setup()
-    gather_finish(0)
     pltpu.make_async_copy(rows, rows_below, setup_recv.at[0]).wait()
     pltpu.make_async_copy(rows, rows_above, setup_recv.at[1]).wait()
     pltpu.make_async_copy(face, face_above, setup_recv.at[2]).wait()
     face_setup()
+    gather_finish(0)
     local_terms(0)
     faces_finish(0)
     join(0, face_terms(0))
     scatter_start(0)
+    scatter_relay(0)
     start = field[0, own_slice()]
     residual = scatter_finish(0) - RIDGE * start
     field[1, own_slice()] = residual
 
     gather_start(1)
+    gather_relay(1)
     gather_finish(1)
     local_terms(1)
     faces_finish(1)
@@ -381,10 +446,12 @@
     square = residual * residual
     sums_start(0, two_sums(square, field[1] * part[1]))
     scatter_start(1)
+    scatter_relay(1)
     sums_second(0)
     image = scatter_finish(1) + RIDGE * field[1, own_slice()]
     field[2, own_slice()] = image
     gather_start(2)
+    gather_relay(2)
     sums_third(0)
 
     gather_finish(2)
@@ -401,6 +468,7 @@
     whole_image = part[1] - step_one * part[2]
     sums_start(1, two_sums(later * later, whole * whole_image))
     scatter_start(2)
+    scatter_relay(2)
     sums_second(1)
     sums_third(1)
     image_two = scatter_finish(2) + RIDGE * field[2, own_slice()]
@@ -414,15 +482,17 @@
     later_image = image - step_one * image_two
     direction = later + beta * residual
     along = later_image + beta * image
-    sol_ref[...] = field[0, own_slice()] + step_one * residual + step_two * direction
-    res_ref[...] = later - step_two * along
+    step_ref[...] = step_one * residual + step_two * direction
+    later_ref[...] = later
+    along_ref[...] = step_two * along
 
     pltpu.make_async_copy(rows, rows, setup_send.at[0]).wait()
     pltpu.make_async_copy(rows, rows, setup_send.at[1]).wait()
     pltpu.make_async_copy(face, face, setup_send.at[2]).wait()
     for step in range(APPLIES):
-        pltpu.make_async_copy(landed.at[step], landed.at[step], gather_send.at[step]).wait()
-        pltpu.make_async_copy(landed.at[step], landed.at[step], scatter_send.at[step]).wait()
+        sent = field.at[step, : (n_bin - 1) * own]
+        pltpu.make_async_copy(sent, sent, gather_send.at[step]).wait()
+        pltpu.make_async_copy(sent, sent, scatter_send.at[step]).wait()
         pltpu.make_async_copy(below.at[step], below.at[step], below_send.at[step]).wait()
         pltpu.make_async_copy(above.at[step], above.at[step], above_send.at[step]).wait()
     for turn in range(2):
@@ -451,8 +521,6 @@
     n_inner = inner_weight.shape[2]
     n_face = face_rows.shape[3]
     part_rows = own * n_bin
-    slots = jnp.arange(n_face, dtype=jnp.int32)
-    listed = jnp.where(slots[None, :] < face_count[0, 0][:, None], face_rows[0, 0], -1)
     half = n_seg // 4
     window = 2 * half - 1
     any_ = pl.BlockSpec(memory_space=pl.ANY)
@@ -461,23 +529,28 @@
     out = jax.ShapeDtypeStruct((own, width), f32)
     call = pl.pallas_call(
         functools.partial(kernel, n_bin, n_seg),
-        out_shape=(out, out),
-        in_specs=[any_] * 10,
-        out_specs=(vmem, vmem),
+        out_shape=(out, out, out),
+        in_specs=[any_] * 11,
+        out_specs=(vmem, vmem, vmem),
         scratch_shapes=[
             pltpu.VMEM((APPLIES, part_rows, width), f32),
             pltpu.VMEM((APPLIES, part_rows, width), f32),
             pltpu.VMEM((APPLIES, part_rows, width), f32),
             pltpu.VMEM((APPLIES, part_rows, width), f32),
-            pltpu.VMEM((APPLIES, n_bin - 1, own, width), f32),
+            pltpu.VMEM((APPLIES, 4, own, width), f32),
+            pltpu.VMEM((APPLIES, 2, own // 2, width), f32),
+            pltpu.VMEM((APPLIES, 2, own, width), f32),
+            pltpu.VMEM((APPLIES, 2, own, width), f32),
             pltpu.VMEM((bin_factors.shape[0] // tile, tile, width), bf16),
             pltpu.VMEM((n_tiles, tile, tile), bf16),
             pltpu.VMEM((n_tiles, tile, tile), bf16),
-            pltpu.SMEM((n_tiles, 2), jnp.int32),
+            pltpu.SMEM((2, n_tiles), jnp.int32),
             pltpu.SMEM((1, 1), jnp.int32),
             pltpu.SMEM((n_inner, 2), jnp.int32),
             pltpu.SMEM((n_tiles + 2 * n_inner, part_rows // tile), f32),
             pltpu.VMEM((n_inner, tile, tile), f32),
+            pltpu.SMEM((1, 2), jnp.int32),
+            pltpu.VMEM((2, n_face), jnp.int32),
             pltpu.VMEM((2, n_face), jnp.int32),
             pltpu.VMEM((2, n_face), jnp.int32),
             pltpu.VMEM((2, n_face), jnp.int32),
@@ -498,7 +571,7 @@
             pltpu.VMEM((2, window, 1, width), f32),
             pltpu.VMEM((2, 2, 1, width), f32),
             pltpu.VMEM((2, n_bin - 1, 1, width), f32),
-            dma((10,)),
+            dma((11,)),
             dma((APPLIES,)),
             dma((APPLIES, n_bin)),
             dma((APPLIES,)),
@@ -506,7 +579,7 @@
             dma((APPLIES,)),
             dma((APPLIES,)),
             dma((APPLIES,)),
-            dma((APPLIES,)),
+            dma((APPLIES, n_bin)),
             dma((3,)),
             dma((3,)),
             dma((2, 3)),
@@ -514,18 +587,20 @@
         ],
         compiler_params=pltpu.CompilerParams(collective_id=0, has_side_effects=True),
     )
-    return call(
+    step, later, along = call(
         start_factors,
         bin_factors.reshape(-1, tile, width),
         tile_speed[0, 0],
         tile_weight[0, 0],
-        tile_cells[0, 0],
+        tile_cells[0, 0].T,
         tile_count,
         inner_pairs[0, 0],
         inner_weight[0, 0],
-        listed,
+        face_rows[0, 0],
+        face_count[0],
         face_weight[0, 0],
     )
+    return start_factors + step, later - along
 
 
 def solution(mesh):

time: 123 us -> 115 us (0.935)
  Pallas kernels: 117 us -> 112 us
  local copies, waits for them, and re-layouts: 3.38 us -> 0.01 us
  other arithmetic: 0.65 us -> 2.01 us
    pallas_call x1, Pallas kernels: 117 us -> 112 us  [shards(): call(start_factors, bin_factors.reshape(-1, tile, width), tile_speed[0, 0...]
    unnamed x10 -> x6, local copies, waits for them, and re-layouts: 2.7 us -> 0.01 us
    add x0 -> x1, other arithmetic: none -> 1.39 us  [shards(): return (start_factors + step, later - along)]
where the time goes in v2:
time: 115 us
  Pallas kernels  112 us (97%)
  other arithmetic  2.01 us (2%)
  between operations  1.32 us (1%)
    pallas_call x1, Pallas kernels, shards(): call(start_factors, bin_factors.reshape(-1, tile, width), tile_speed[0, 0...  112 us

profile of v2, /device:TPU:80, one launch (start us, length us, event | category | flops | bytes accessed | tf_op | source)
XLA Modules:
  0.0 115.0 jit_solution(11236636667140950229)
XLA Ops:
  1.3 0.0 copy-start
  1.3 111.6 %shard_map.122 = (f32[64,128]{1,0:T(8,128)}, f32[64,128]{1,0:T(8,128)}, f32[64,128]{1,0:T(8,128)}) custom-call(f32[64,128]{1,0:T(8,128)} %x0_hbm.1, bf16[8,128,128]{2,1,0:T(8,128)(2,1)} %bitcast.13, bf16[12,128,128]{2,1,0:T(8,128)(2,1)} %bitcast.11, bf16[12,128,128]{2,1,0:T(8,128)(2,1)} %bitcast.12, s32[2,12]{1,0:T(2,128)} %bitcast.17, ...), custom_call_target="tpu_custom_call" | custom-call | tf_op jit(solution)/shard_map/pallas_call | solution.py:590
  112.9 0.0 copy-done
  112.9 0.0 copy-start.1
  112.9 0.0 copy-start.2
  113.0 1.4 %add.3 = f32[64,128]{1,0:T(8,128)} add(f32[64,128]{1,0:T(8,128)S(1)} %copy-done, f32[64,128]{1,0:T(8,128)} %get-tuple-element.5) | non-fusion elementwise | flops 8192 | bytes 98304 | tf_op jit(solution)/shard_map/add | solution.py:603
  114.3 0.0 copy-done.1
  114.3 0.0 copy-done.2
  114.3 0.6 sub.3
Async XLA Ops:
  1.3 111.6 %copy-start = (f32[64,128]{1,0:T(8,128)S(1)}, f32[64,128]{1,0:T(8,128)}, u32[]{:S(2)}) copy-start(f32[64,128]{1,0:T(8,128)} %x0_hbm.1) | copy-start | bytes 98308
  112.9 1.4 %copy-start.1 = (f32[64,128]{1,0:T(8,128)S(1)}, f32[64,128]{1,0:T(8,128)}, u32[]{:S(2)}) copy-start(f32[64,128]{1,0:T(8,128)} %get-tuple-element.6) | copy-start | bytes 98308
  112.9 1.4 %copy-start.2 = (f32[64,128]{1,0:T(8,128)S(1)}, f32[64,128]{1,0:T(8,128)}, u32[]{:S(2)}) copy-start(f32[64,128]{1,0:T(8,128)} %get-tuple-element.7) | copy-start | bytes 98308

commit v3 on v2

--- a/solution.py
+++ b/solution.py
@@ -41,9 +41,8 @@
     rows_hbm,
     lives_hbm,
     face_hbm,
-    step_ref,
-    later_ref,
-    along_ref,
+    sol_ref,
+    res_ref,
     field,
     below,
     above,
@@ -52,6 +51,7 @@
     halves,
     fulls,
     passed,
+    summed,
     bins,
     speed,
     weight,
@@ -77,10 +77,12 @@
     f_above,
     degree,
     rhs,
+    base,
     wide,
     sums_mine,
     sums_seg,
     sums_far,
+    sums_all,
     sums_bin,
     load_sem,
     gather_send,
@@ -244,23 +246,23 @@
                 product = product + dot_nn(w_lo[2 * j + way], picked[:, :width])
                 pulled[n_tiles + 2 * j + way] = -product
 
-    def face_terms(step):
-        total = None
-        for matrix, source in ((f_below, below), (f_above, above)):
-            hi, lo = split(source[step])
-            both = jnp.concatenate([hi, lo], axis=1)
-            product = doubled(dot_nn(matrix[0], both)) + dot_nn(matrix[1], hi)
-            total = product if total is None else total + product
-        return total
-
-    def join(step, faces):
+    def face_term(step, matrix, source):
+        hi, lo = split(source[step])
+        both = jnp.concatenate([hi, lo], axis=1)
+        return doubled(dot_nn(matrix[0], both)) + dot_nn(matrix[1], hi)
+
+    def base_terms(step):
         items = [((lambda k=k: pulled[k]), k) for k in range(n_tiles)]
         for j in range(2 * n_inner):
             items.append(((lambda j=j: pulled[n_tiles + j]), n_tiles + j))
         for b in range(n_blocks):
             at = slice(b * tile, (b + 1) * tile)
-            value = add_up(items, b) + degree[at] * field[step, at] - faces[at]
-            part[step, at] = rhs[at] - value if step == 0 else value
+            value = add_up(items, b) + degree[at] * field[step, at]
+            base[at] = value
+
+    def join(step, faces):
+        value = base[...] - faces
+        part[step] = rhs[...] - value if step == 0 else value
 
     order = sorted(range(1, n_bin), key=lambda d: -min(d, n_bin - d))
 
@@ -276,13 +278,10 @@
             device_id={"seg": where}, device_id_type=MESH,
         )
 
-    def forward(step, source):
-        rows_at = pl.ds(pl.multiple_of(source * own, own), own)
-        block = field.at[step, rows_at]
-        to_seg(block, below.at[step, rows_at], below_send.at[step], below_recv.at[step], seg_next).start()
-        to_seg(block, above.at[step, rows_at], above_send.at[step], above_recv.at[step], seg_prev).start()
-
+    direct = lax.rem(seg, 2) == 0
+    tree = jnp.logical_not(direct)
     slot_of = {-1: 0, 1: 1, -2: 2, 2: 3, -3: 4, 3: 5, -4: 6, 4: 7}
+    straight = (4, 3, -3, 2, -2, 1, -1)
 
     def block_rows(offset, part_of=None):
         at = lax.rem(bin_ + (offset + n_bin), n_bin) * own
@@ -296,74 +295,131 @@
         recv = gather_recv.at[step, slot_of[source - to]]
         to_bin(block, block, gather_send.at[step], recv, to + n_bin).start()
 
-    def gather_wait(step, source, part_of=None):
+    def gather_take(step, source, part_of=None):
         block = field.at[step, block_rows(source, part_of)]
         pltpu.make_async_copy(block, block, gather_recv.at[step, slot_of[source]]).wait()
+
+    def pass_on(step, source, part_of=None):
         rows_at = block_rows(source, part_of)
+        block = field.at[step, rows_at]
         to_seg(block, below.at[step, rows_at], below_send.at[step], below_recv.at[step], seg_next).start()
         to_seg(block, above.at[step, rows_at], above_send.at[step], above_recv.at[step], seg_prev).start()
 
     def gather_start(step):
-        for to in (2, -2, 1, -1):
-            gather_send_to(step, 0, to)
-        forward(step, bin_)
+        @pl.when(direct)
+        def _():
+            for to in straight:
+                gather_send_to(step, 0, to)
+
+        @pl.when(tree)
+        def _():
+            for to in (2, -2, 1, -1):
+                gather_send_to(step, 0, to)
+
+        pass_on(step, 0)
 
     def gather_relay(step):
-        for side in (-1, 1):
-            source = 2 * side
-            block = field.at[step, block_rows(source)]
-            pltpu.make_async_copy(block, block, gather_recv.at[step, slot_of[source]]).wait()
-            gather_send_to(step, source, -side)
-            gather_send_to(step, source, -2 * side, 0 if side < 0 else 1)
-            forward(step, lax.rem(bin_ + (source + n_bin), n_bin))
-        gather_wait(step, -1)
-        gather_wait(step, 1)
+        @pl.when(direct)
+        def _():
+            for source in (3, 2, -3, -2):
+                gather_take(step, source)
+                pass_on(step, source)
+
+        @pl.when(tree)
+        def _():
+            for side in (-1, 1):
+                source = 2 * side
+                gather_take(step, source)
+                gather_send_to(step, source, -side)
+                gather_send_to(step, source, -2 * side, 0 if side < 0 else 1)
+                pass_on(step, source)
+            for source in (-1, 1):
+                gather_take(step, source)
+                pass_on(step, source)
 
     def gather_finish(step):
-        gather_wait(step, -3)
-        gather_wait(step, 3)
-        gather_wait(step, -4, 0)
-        gather_wait(step, 4, 1)
-
-    def faces_finish(step):
-        pltpu.make_async_copy(below.at[step], below.at[step], below_recv.at[step]).wait()
-        pltpu.make_async_copy(above.at[step], above.at[step], above_recv.at[step]).wait()
+        @pl.when(direct)
+        def _():
+            for source in (1, -1, -4):
+                gather_take(step, source)
+                pass_on(step, source)
+
+        @pl.when(tree)
+        def _():
+            for source, part_of in ((-3, None), (3, None), (-4, 0), (4, 1)):
+                gather_take(step, source, part_of)
+                pass_on(step, source, part_of)
+
+    def faces_join(step):
+        def one(matrix, source, recv):
+            pltpu.make_async_copy(source.at[step], source.at[step], recv.at[step]).wait()
+            return face_term(step, matrix, source)
+
+        @pl.when(direct)
+        def _():
+            base[...] -= one(f_above, above, above_recv)
+            join(step, one(f_below, below, below_recv))
+
+        @pl.when(tree)
+        def _():
+            base[...] -= one(f_below, below, below_recv)
+            join(step, one(f_above, above, above_recv))
 
     def scatter_send_to(step, src, dst, slot, to):
         to_bin(src, dst, scatter_send.at[step], scatter_recv.at[step, slot], to + n_bin).start()
 
     def scatter_start(step):
-        for side in (-1, 1):
-            at = 0 if side < 0 else 1
-            scatter_send_to(step, part.at[step, block_rows(4, 1 - at)], halves.at[step, at], at, 2 * side)
-            scatter_send_to(step, part.at[step, block_rows(3 * side)], fulls.at[step, at], 2 + at, side)
-        for side in (-1, 1):
-            at = 0 if side < 0 else 1
-            scatter_send_to(step, part.at[step, block_rows(side)], landed.at[step, at], 4 + at, side)
+        @pl.when(direct)
+        def _():
+            for slot, to in enumerate(straight):
+                block = part.at[step, block_rows(to)]
+                scatter_send_to(step, block, landed.at[step, slot], slot, to)
+
+        @pl.when(tree)
+        def _():
+            for at, side in enumerate((-1, 1)):
+                far = part.at[step, block_rows(4, 1 - at)]
+                scatter_send_to(step, far, halves.at[step, at], 4 + at, 2 * side)
+                near = part.at[step, block_rows(3 * side)]
+                scatter_send_to(step, near, fulls.at[step, at], 6 + at, side)
+            for at, side in enumerate((-1, 1)):
+                block = part.at[step, block_rows(side)]
+                scatter_send_to(step, block, landed.at[step, at], at, side)
 
     def arrived(step, ref, slot):
         pltpu.make_async_copy(ref, ref, scatter_recv.at[step, slot]).wait()
 
     def scatter_relay(step):
-        for side in (-1, 1):
-            at = 0 if side < 0 else 1
+        @pl.when(tree)
+        def _():
             size = own // 2
-            arrived(step, fulls.at[step, at], 2 + at)
-            arrived(step, halves.at[step, at], at)
-            total = part[step, block_rows(2 * side)] + fulls[step, at]
-            other = 1 - at
-            mine = slice(other * size, (other + 1) * size)
-            rest = slice(at * size, (at + 1) * size)
-            passed[step, at, rest] = total[rest]
-            passed[step, at, mine] = total[mine] + halves[step, at]
-            scatter_send_to(step, passed.at[step, at], landed.at[step, 2 + at], 6 + at, 2 * side)
+            for at, side in enumerate((-1, 1)):
+                arrived(step, fulls.at[step, at], 6 + at)
+                arrived(step, halves.at[step, at], 4 + at)
+                total = part[step, block_rows(2 * side)] + fulls[step, at]
+                mine = slice((1 - at) * size, (2 - at) * size)
+                rest = slice(at * size, (at + 1) * size)
+                passed[step, at, rest] = total[rest]
+                passed[step, at, mine] = total[mine] + halves[step, at]
+                scatter_send_to(step, passed.at[step, at], landed.at[step, 2 + at], 2 + at, 2 * side)
 
     def scatter_finish(step):
-        total = part[step, own_slice()]
-        for at in range(4):
-            arrived(step, landed.at[step, at], 4 + at)
-            total = total + landed[step, at]
-        return total
+        def add(slots):
+            total = part[step, own_slice()]
+            for slot in slots:
+                arrived(step, landed.at[step, slot], slot)
+                total = total + landed[step, slot]
+            summed[...] = total
+
+        @pl.when(direct)
+        def _():
+            add(range(len(straight) - 1, -1, -1))
+
+        @pl.when(tree)
+        def _():
+            add(range(4))
+
+        return summed[...]
 
     window = [e for e in range(-half + 1, half + 1) if e != 0]
 
@@ -378,20 +434,34 @@
     def sums_start(turn, value):
         sums_mine[turn, 0] = value
         for at, e in enumerate(window):
-            to_seg(sums_mine.at[turn, 0], sums_seg.at[turn, at], sums_send.at[turn, 0], sums_recv.at[turn, 0], seg_at(e)).start()
+            to_seg(sums_mine.at[turn, 0], sums_seg.at[at], sums_send.at[turn, 0], sums_recv.at[turn, 0], seg_at(e)).start()
 
     def sums_second(turn):
-        pltpu.make_async_copy(sums_seg.at[turn], sums_seg.at[turn], sums_recv.at[turn, 0]).wait()
+        pltpu.make_async_copy(sums_seg, sums_seg, sums_recv.at[turn, 0]).wait()
         total = sums_mine[turn, 0]
         for at in range(len(window)):
-            total = total + sums_seg[turn, at]
+            total = total + sums_seg[at]
         sums_mine[turn, 1] = total
         for at, e in enumerate((-half, half)):
-            to_seg(sums_mine.at[turn, 1], sums_far.at[turn, at], sums_send.at[turn, 1], sums_recv.at[turn, 1], seg_at(e)).start()
+            to_seg(sums_mine.at[turn, 1], sums_far.at[at], sums_send.at[turn, 1], sums_recv.at[turn, 1], seg_at(e)).start()
 
     def sums_third(turn):
-        pltpu.make_async_copy(sums_far.at[turn], sums_far.at[turn], sums_recv.at[turn, 1]).wait()
-        total = sums_far[turn, 0] + sums_far[turn, 1]
+        pltpu.make_async_copy(sums_far, sums_far, sums_recv.at[turn, 1]).wait()
+        sums_to_bins(turn, sums_far[0] + sums_far[1])
+
+    def sums_start_all(turn, value):
+        sums_mine[turn, 0] = value
+        for e in sorted(range(1, n_seg), key=lambda e: -min(e, n_seg - e)):
+            to_seg(sums_mine.at[turn, 0], sums_all.at[e - 1], sums_send.at[turn, 0], sums_recv.at[turn, 0], seg_at(e)).start()
+
+    def sums_third_all(turn):
+        pltpu.make_async_copy(sums_all, sums_all, sums_recv.at[turn, 0]).wait()
+        total = sums_mine[turn, 0]
+        for e in range(1, n_seg):
+            total = total + sums_all[e - 1]
+        sums_to_bins(turn, total)
+
+    def sums_to_bins(turn, total):
         sums_mine[turn, 2] = total
         for d in order:
             to_bin(sums_mine.at[turn, 2], sums_bin.at[turn, d - 1], sums_send.at[turn, 2], sums_recv.at[turn, 2], d).start()
@@ -413,10 +483,10 @@
         own_list = listed[side : side + 1, :]
         rows[side : side + 1, :] = jnp.where(slot_at < lives[0, side], own_list, -1)
     loads[0].wait()
+    pl.semaphore_wait(barrier, n_bin - 1 + len(seg_offsets))
+    gather_start(0)
     loads[3].wait()
-    pl.semaphore_wait(barrier, n_bin - 1 + len(seg_offsets))
     to_seg(face, face_above, setup_send.at[2], setup_recv.at[2], seg_prev).start()
-    gather_start(0)
     to_seg(rows, rows_below, setup_send.at[0], setup_recv.at[0], seg_next).start()
     to_seg(rows, rows_above, setup_send.at[1], setup_recv.at[1], seg_prev).start()
     slots_and_gain()
@@ -429,8 +499,8 @@
     face_setup()
     gather_finish(0)
     local_terms(0)
-    faces_finish(0)
-    join(0, face_terms(0))
+    base_terms(0)
+    faces_join(0)
     scatter_start(0)
     scatter_relay(0)
     start = field[0, own_slice()]
@@ -441,11 +511,11 @@
     gather_relay(1)
     gather_finish(1)
     local_terms(1)
-    faces_finish(1)
-    join(1, face_terms(1))
+    base_terms(1)
+    faces_join(1)
     square = residual * residual
+    scatter_start(1)
     sums_start(0, two_sums(square, field[1] * part[1]))
-    scatter_start(1)
     scatter_relay(1)
     sums_second(0)
     image = scatter_finish(1) + RIDGE * field[1, own_slice()]
@@ -456,8 +526,8 @@
 
     gather_finish(2)
     local_terms(2)
-    faces_finish(2)
-    join(2, face_terms(2))
+    base_terms(2)
+    faces_join(2)
     norm, product = sums_finish(0)
     product = product + RIDGE * norm
     step_one = norm / product
@@ -466,11 +536,10 @@
     later = residual - step_one * image
     whole = field[1] - step_one * field[2]
     whole_image = part[1] - step_one * part[2]
-    sums_start(1, two_sums(later * later, whole * whole_image))
+    sums_start_all(1, two_sums(later * later, whole * whole_image))
     scatter_start(2)
     scatter_relay(2)
-    sums_second(1)
-    sums_third(1)
+    sums_third_all(1)
     image_two = scatter_finish(2) + RIDGE * field[2, own_slice()]
     norm_next, product_next = sums_finish(1)
     product_next = product_next + RIDGE * norm_next
@@ -482,9 +551,8 @@
     later_image = image - step_one * image_two
     direction = later + beta * residual
     along = later_image + beta * image
-    step_ref[...] = step_one * residual + step_two * direction
-    later_ref[...] = later
-    along_ref[...] = step_two * along
+    sol_ref[...] = field[0, own_slice()] + step_one * residual + step_two * direction
+    res_ref[...] = later - step_two * along
 
     pltpu.make_async_copy(rows, rows, setup_send.at[0]).wait()
     pltpu.make_async_copy(rows, rows, setup_send.at[1]).wait()
@@ -495,9 +563,10 @@
         pltpu.make_async_copy(sent, sent, scatter_send.at[step]).wait()
         pltpu.make_async_copy(below.at[step], below.at[step], below_send.at[step]).wait()
         pltpu.make_async_copy(above.at[step], above.at[step], above_send.at[step]).wait()
+    pltpu.make_async_copy(sums_seg, sums_seg, sums_send.at[0, 0]).wait()
+    pltpu.make_async_copy(sums_far, sums_far, sums_send.at[0, 1]).wait()
+    pltpu.make_async_copy(sums_all, sums_all, sums_send.at[1, 0]).wait()
     for turn in range(2):
-        pltpu.make_async_copy(sums_seg.at[turn], sums_seg.at[turn], sums_send.at[turn, 0]).wait()
-        pltpu.make_async_copy(sums_far.at[turn], sums_far.at[turn], sums_send.at[turn, 1]).wait()
         pltpu.make_async_copy(sums_bin.at[turn], sums_bin.at[turn], sums_send.at[turn, 2]).wait()
 
 
@@ -526,21 +595,21 @@
     any_ = pl.BlockSpec(memory_space=pl.ANY)
     vmem = pl.BlockSpec(memory_space=pltpu.VMEM)
     dma = pltpu.SemaphoreType.DMA
-    out = jax.ShapeDtypeStruct((own, width), f32)
     call = pl.pallas_call(
         functools.partial(kernel, n_bin, n_seg),
-        out_shape=(out, out, out),
+        out_shape=(pltpu.VMEM((own, width), f32),) * 2,
         in_specs=[any_] * 11,
-        out_specs=(vmem, vmem, vmem),
+        out_specs=(vmem, vmem),
         scratch_shapes=[
             pltpu.VMEM((APPLIES, part_rows, width), f32),
             pltpu.VMEM((APPLIES, part_rows, width), f32),
             pltpu.VMEM((APPLIES, part_rows, width), f32),
             pltpu.VMEM((APPLIES, part_rows, width), f32),
-            pltpu.VMEM((APPLIES, 4, own, width), f32),
+            pltpu.VMEM((APPLIES, 7, own, width), f32),
             pltpu.VMEM((APPLIES, 2, own // 2, width), f32),
             pltpu.VMEM((APPLIES, 2, own, width), f32),
             pltpu.VMEM((APPLIES, 2, own, width), f32),
+            pltpu.VMEM((own, width), f32),
             pltpu.VMEM((bin_factors.shape[0] // tile, tile, width), bf16),
             pltpu.VMEM((n_tiles, tile, tile), bf16),
             pltpu.VMEM((n_tiles, tile, tile), bf16),
@@ -566,10 +635,12 @@
             pltpu.VMEM((2, part_rows, part_rows), bf16),
             pltpu.VMEM((part_rows, width), f32),
             pltpu.VMEM((part_rows, width), f32),
+            pltpu.VMEM((part_rows, width), f32),
             pltpu.VMEM((part_rows // tile, tile, 2 * width), bf16),
             pltpu.VMEM((2, 3, 1, width), f32),
-            pltpu.VMEM((2, window, 1, width), f32),
-            pltpu.VMEM((2, 2, 1, width), f32),
+            pltpu.VMEM((window, 1, width), f32),
+            pltpu.VMEM((2, 1, width), f32),
+            pltpu.VMEM((n_seg - 1, 1, width), f32),
             pltpu.VMEM((2, n_bin - 1, 1, width), f32),
             dma((11,)),
             dma((APPLIES,)),
@@ -587,7 +658,7 @@
         ],
         compiler_params=pltpu.CompilerParams(collective_id=0, has_side_effects=True),
     )
-    step, later, along = call(
+    return call(
         start_factors,
         bin_factors.reshape(-1, tile, width),
         tile_speed[0, 0],
@@ -600,7 +671,6 @@
         face_count[0],
         face_weight[0, 0],
     )
-    return start_factors + step, later - along
 
 
 def solution(mesh):

time: 115 us -> 110 us (0.957)
  Pallas kernels: 112 us -> 107 us
  other arithmetic: 2.01 us -> 0 us
  local copies, waits for them, and re-layouts: 0.01 us -> 1.23 us
    pallas_call x1, Pallas kernels: 112 us -> 107 us  [shards(): call(start_factors, bin_factors.reshape(-1, tile, width), tile_speed[0, 0...]
    add x1 -> x0, other arithmetic: 1.39 us -> none  [shards(): return (start_factors + step, later - along)]
    unnamed x6 -> x2, local copies, waits for them, and re-layouts: 0.01 us -> 1.23 us
where the time goes in v3:
time: 110 us; the launch traced here: 109 us
  Pallas kernels  107 us (97%)
  between operations  1.29 us (1%)
  local copies, waits for them, and re-layouts  1.23 us (1%)
    pallas_call x1, Pallas kernels, shards(): call(start_factors, bin_factors.reshape(-1, tile, width), tile_speed[0, 0...  107 us

profile of v3, /device:TPU:80, one launch (start us, length us, event | category | flops | bytes accessed | tf_op | source)
XLA Modules:
  0.0 109.4 jit_solution(15298101520142586046)
XLA Ops:
  1.3 106.8 %shard_map.122 = (f32[64,128]{1,0:T(8,128)S(1)}, f32[64,128]{1,0:T(8,128)S(1)}) custom-call(f32[64,128]{1,0:T(8,128)} %x0_hbm.1, bf16[8,128,128]{2,1,0:T(8,128)(2,1)} %bitcast.13, bf16[12,128,128]{2,1,0:T(8,128)(2,1)} %bitcast.11, bf16[12,128,128]{2,1,0:T(8,128)(2,1)} %bitcast.12, s32[2,12]{1,0:T(2,128)} %bitcast.17, s32[1,1]{1,0:T(1,128)S(6)} %copy.17.count_hbm, ...), custom_call_target="tpu_custom_call" | custom-call | tf_op jit(solution)/shard_map/pallas_call | solution.py:661
  108.1 0.6 copy.15
  108.7 0.6 copy.16

commit v4 on v3

--- a/solution.py
+++ b/solution.py
@@ -9,6 +9,7 @@
 
 RIDGE = 0.5
 APPLIES = 3
+WAVES = 2
 MESH = pl.DeviceIdType.MESH
 f32 = jnp.float32
 bf16 = jnp.bfloat16
@@ -52,6 +53,7 @@
     fulls,
     passed,
     summed,
+    last,
     bins,
     speed,
     weight,
@@ -78,6 +80,7 @@
     degree,
     rhs,
     base,
+    whole,
     wide,
     sums_mine,
     sums_seg,
@@ -282,73 +285,77 @@
     tree = jnp.logical_not(direct)
     slot_of = {-1: 0, 1: 1, -2: 2, 2: 3, -3: 4, 3: 5, -4: 6, 4: 7}
     straight = (4, 3, -3, 2, -2, 1, -1)
-
-    def block_rows(offset, part_of=None):
-        at = lax.rem(bin_ + (offset + n_bin), n_bin) * own
-        size = own if part_of is None else own // 2
+    wave_rows = own // WAVES
+
+    def block_rows(wave, offset, part_of=None):
+        at = lax.rem(bin_ + (offset + n_bin), n_bin) * own + wave * wave_rows
+        size = wave_rows if part_of is None else wave_rows // 2
         if part_of:
             at = at + size
         return pl.ds(pl.multiple_of(at, size), size)
 
-    def gather_send_to(step, source, to, part_of=None):
-        block = field.at[step, block_rows(source, part_of)]
-        recv = gather_recv.at[step, slot_of[source - to]]
+    def gather_send_to(step, wave, source, to, part_of=None):
+        block = field.at[step, block_rows(wave, source, part_of)]
+        recv = gather_recv.at[step, wave, slot_of[source - to]]
         to_bin(block, block, gather_send.at[step], recv, to + n_bin).start()
 
-    def gather_take(step, source, part_of=None):
-        block = field.at[step, block_rows(source, part_of)]
-        pltpu.make_async_copy(block, block, gather_recv.at[step, slot_of[source]]).wait()
-
-    def pass_on(step, source, part_of=None):
-        rows_at = block_rows(source, part_of)
+    def gather_take(step, wave, source, part_of=None):
+        block = field.at[step, block_rows(wave, source, part_of)]
+        pltpu.make_async_copy(block, block, gather_recv.at[step, wave, slot_of[source]]).wait()
+
+    def pass_on(step, wave, source, part_of=None):
+        rows_at = block_rows(wave, source, part_of)
         block = field.at[step, rows_at]
         to_seg(block, below.at[step, rows_at], below_send.at[step], below_recv.at[step], seg_next).start()
         to_seg(block, above.at[step, rows_at], above_send.at[step], above_recv.at[step], seg_prev).start()
 
-    def gather_start(step):
+    def gather_start(step, wave):
         @pl.when(direct)
         def _():
             for to in straight:
-                gather_send_to(step, 0, to)
+                gather_send_to(step, wave, 0, to)
 
         @pl.when(tree)
         def _():
             for to in (2, -2, 1, -1):
-                gather_send_to(step, 0, to)
-
-        pass_on(step, 0)
+                gather_send_to(step, wave, 0, to)
+
+        pass_on(step, wave, 0)
 
     def gather_relay(step):
         @pl.when(direct)
         def _():
-            for source in (3, 2, -3, -2):
-                gather_take(step, source)
-                pass_on(step, source)
+            for source in (3, 2, -3, -2, 1, -1, -4):
+                gather_take(step, 0, source)
+                pass_on(step, 0, source)
 
         @pl.when(tree)
         def _():
-            for side in (-1, 1):
-                source = 2 * side
-                gather_take(step, source)
-                gather_send_to(step, source, -side)
-                gather_send_to(step, source, -2 * side, 0 if side < 0 else 1)
-                pass_on(step, source)
-            for source in (-1, 1):
-                gather_take(step, source)
-                pass_on(step, source)
+            for wave in range(WAVES):
+                for side in (-1, 1):
+                    source = 2 * side
+                    gather_take(step, wave, source)
+                    gather_send_to(step, wave, source, -side)
+                    gather_send_to(step, wave, source, -2 * side, 0 if side < 0 else 1)
+                    pass_on(step, wave, source)
+                for source in (-1, 1):
+                    gather_take(step, wave, source)
+                    pass_on(step, wave, source)
 
     def gather_finish(step):
         @pl.when(direct)
         def _():
-            for source in (1, -1, -4):
-                gather_take(step, source)
-                pass_on(step, source)
+            for wave in range(1, WAVES):
+                for source in (3, 2, -3, -2, 1, -1, -4):
+                    gather_take(step, wave, source)
+                    pass_on(step, wave, source)
 
         @pl.when(tree)
         def _():
-            for source, part_of in ((-3, None), (3, None), (-4, 0), (4, 1)):
-                gather_take(step, source, part_of)
-                pass_on(step, source, part_of)
+            for wave in range(WAVES):
+                for source, part_of in ((-3, None), (3, None), (-4, 0), (4, 1)):
+                    gather_take(step, wave, source, part_of)
+                    pass_on(step, wave, source, part_of)
 
     def faces_join(step):
         def one(matrix, source, recv):
@@ -365,50 +372,53 @@
             base[...] -= one(f_below, below, below_recv)
             join(step, one(f_above, above, above_recv))
 
-    def scatter_send_to(step, src, dst, slot, to):
-        to_bin(src, dst, scatter_send.at[step], scatter_recv.at[step, slot], to + n_bin).start()
+    def scatter_send_to(step, wave, src, dst, slot, to):
+        to_bin(src, dst, scatter_send.at[step], scatter_recv.at[step, wave, slot], to + n_bin).start()
 
     def scatter_start(step):
-        @pl.when(direct)
-        def _():
-            for slot, to in enumerate(straight):
-                block = part.at[step, block_rows(to)]
-                scatter_send_to(step, block, landed.at[step, slot], slot, to)
-
-        @pl.when(tree)
-        def _():
-            for at, side in enumerate((-1, 1)):
-                far = part.at[step, block_rows(4, 1 - at)]
-                scatter_send_to(step, far, halves.at[step, at], 4 + at, 2 * side)
-                near = part.at[step, block_rows(3 * side)]
-                scatter_send_to(step, near, fulls.at[step, at], 6 + at, side)
-            for at, side in enumerate((-1, 1)):
-                block = part.at[step, block_rows(side)]
-                scatter_send_to(step, block, landed.at[step, at], at, side)
-
-    def arrived(step, ref, slot):
-        pltpu.make_async_copy(ref, ref, scatter_recv.at[step, slot]).wait()
+        for wave in range(WAVES):
+            @pl.when(direct)
+            def _():
+                for slot, to in enumerate(straight):
+                    block = part.at[step, block_rows(wave, to)]
+                    scatter_send_to(step, wave, block, landed.at[step, wave, slot], slot, to)
+
+            @pl.when(tree)
+            def _():
+                for at, side in enumerate((-1, 1)):
+                    far = part.at[step, block_rows(wave, 4, 1 - at)]
+                    scatter_send_to(step, wave, far, halves.at[step, wave, at], 4 + at, 2 * side)
+                    near = part.at[step, block_rows(wave, 3 * side)]
+                    scatter_send_to(step, wave, near, fulls.at[step, wave, at], 6 + at, side)
+                for at, side in enumerate((-1, 1)):
+                    block = part.at[step, block_rows(wave, side)]
+                    scatter_send_to(step, wave, block, landed.at[step, wave, at], at, side)
+
+    def arrived(step, wave, ref, slot):
+        pltpu.make_async_copy(ref, ref, scatter_recv.at[step, wave, slot]).wait()
 
     def scatter_relay(step):
         @pl.when(tree)
         def _():
-            size = own // 2
-            for at, side in enumerate((-1, 1)):
-                arrived(step, fulls.at[step, at], 6 + at)
-                arrived(step, halves.at[step, at], 4 + at)
-                total = part[step, block_rows(2 * side)] + fulls[step, at]
-                mine = slice((1 - at) * size, (2 - at) * size)
-                rest = slice(at * size, (at + 1) * size)
-                passed[step, at, rest] = total[rest]
-                passed[step, at, mine] = total[mine] + halves[step, at]
-                scatter_send_to(step, passed.at[step, at], landed.at[step, 2 + at], 2 + at, 2 * side)
-
-    def scatter_finish(step):
+            size = wave_rows // 2
+            for wave in range(WAVES):
+                for at, side in enumerate((-1, 1)):
+                    arrived(step, wave, fulls.at[step, wave, at], 6 + at)
+                    arrived(step, wave, halves.at[step, wave, at], 4 + at)
+                    total = part[step, block_rows(wave, 2 * side)] + fulls[step, wave, at]
+                    mine = slice((1 - at) * size, (2 - at) * size)
+                    rest = slice(at * size, (at + 1) * size)
+                    passed[step, wave, at, rest] = total[rest]
+                    passed[step, wave, at, mine] = total[mine] + halves[step, wave, at]
+                    dst = landed.at[step, wave, 2 + at]
+                    scatter_send_to(step, wave, passed.at[step, wave, at], dst, 2 + at, 2 * side)
+
+    def scatter_finish(step, wave):
         def add(slots):
-            total = part[step, own_slice()]
+            total = part[step, block_rows(wave, 0)]
             for slot in slots:
-                arrived(step, landed.at[step, slot], slot)
-                total = total + landed[step, slot]
+                arrived(step, wave, landed.at[step, wave, slot], slot)
+                total = total + landed[step, wave, slot]
             summed[...] = total
 
         @pl.when(direct)
@@ -476,15 +486,16 @@
         second = jnp.sum(jnp.where(lanes < width // 2, 0.0, total), axis=1, keepdims=True)
         return first, second
 
+    loads[0].wait()
+    pl.semaphore_wait(barrier, n_bin - 1 + len(seg_offsets))
+    for wave in range(WAVES):
+        gather_start(0, wave)
     for load in loads[1:3]:
         load.wait()
     slot_at = lax.broadcasted_iota(jnp.int32, (1, listed.shape[1]), 1)
     for side in range(2):
         own_list = listed[side : side + 1, :]
         rows[side : side + 1, :] = jnp.where(slot_at < lives[0, side], own_list, -1)
-    loads[0].wait()
-    pl.semaphore_wait(barrier, n_bin - 1 + len(seg_offsets))
-    gather_start(0)
     loads[3].wait()
     to_seg(face, face_above, setup_send.at[2], setup_recv.at[2], seg_prev).start()
     to_seg(rows, rows_below, setup_send.at[0], setup_recv.at[0], seg_next).start()
@@ -503,44 +514,50 @@
     faces_join(0)
     scatter_start(0)
     scatter_relay(0)
-    start = field[0, own_slice()]
-    residual = scatter_finish(0) - RIDGE * start
-    field[1, own_slice()] = residual
-
-    gather_start(1)
+    for wave in range(WAVES):
+        mine = block_rows(wave, 0)
+        field[1, mine] = scatter_finish(0, wave) - RIDGE * field[0, mine]
+        gather_start(1, wave)
+
     gather_relay(1)
     gather_finish(1)
     local_terms(1)
     base_terms(1)
     faces_join(1)
+    residual = field[1, own_slice()]
     square = residual * residual
     scatter_start(1)
     sums_start(0, two_sums(square, field[1] * part[1]))
     scatter_relay(1)
-    sums_second(0)
-    image = scatter_finish(1) + RIDGE * field[1, own_slice()]
-    field[2, own_slice()] = image
-    gather_start(2)
+    for wave in range(WAVES):
+        mine = block_rows(wave, 0)
+        field[2, mine] = scatter_finish(1, wave) + RIDGE * field[1, mine]
+        gather_start(2, wave)
+        if wave == 0:
+            sums_second(0)
     gather_relay(2)
     sums_third(0)
 
     gather_finish(2)
     local_terms(2)
     base_terms(2)
-    faces_join(2)
     norm, product = sums_finish(0)
     product = product + RIDGE * norm
     step_one = norm / product
     residual = field[1, own_slice()]
     image = field[2, own_slice()]
     later = residual - step_one * image
-    whole = field[1] - step_one * field[2]
+    later_square = (later * later).sum(0, keepdims=True)
+    whole[...] = field[1] - step_one * field[2]
+    faces_join(2)
     whole_image = part[1] - step_one * part[2]
-    sums_start_all(1, two_sums(later * later, whole * whole_image))
+    sums_start_all(1, two_sums(later_square, whole[...] * whole_image))
     scatter_start(2)
     scatter_relay(2)
     sums_third_all(1)
-    image_two = scatter_finish(2) + RIDGE * field[2, own_slice()]
+    for wave in range(WAVES):
+        mine = block_rows(wave, 0)
+        last[wave * wave_rows : (wave + 1) * wave_rows] = scatter_finish(2, wave) + RIDGE * field[2, mine]
     norm_next, product_next = sums_finish(1)
     product_next = product_next + RIDGE * norm_next
     beta = norm_next / norm
@@ -548,7 +565,7 @@
     residual = field[1, own_slice()]
     image = field[2, own_slice()]
     later = residual - step_one * image
-    later_image = image - step_one * image_two
+    later_image = image - step_one * last[...]
     direction = later + beta * residual
     along = later_image + beta * image
     sol_ref[...] = field[0, own_slice()] + step_one * residual + step_two * direction
@@ -568,6 +585,11 @@
     pltpu.make_async_copy(sums_all, sums_all, sums_send.at[1, 0]).wait()
     for turn in range(2):
         pltpu.make_async_copy(sums_bin.at[turn], sums_bin.at[turn], sums_send.at[turn, 2]).wait()
+
+
+def finish_kernel(sol_in, res_in, sol_ref, res_ref):
+    sol_ref[...] = sol_in[...]
+    res_ref[...] = res_in[...]
 
 
 def shards(
@@ -605,10 +627,11 @@
             pltpu.VMEM((APPLIES, part_rows, width), f32),
             pltpu.VMEM((APPLIES, part_rows, width), f32),
             pltpu.VMEM((APPLIES, part_rows, width), f32),
-            pltpu.VMEM((APPLIES, 7, own, width), f32),
-            pltpu.VMEM((APPLIES, 2, own // 2, width), f32),
-            pltpu.VMEM((APPLIES, 2, own, width), f32),
-            pltpu.VMEM((APPLIES, 2, own, width), f32),
+            pltpu.VMEM((APPLIES, WAVES, 7, own // WAVES, width), f32),
+            pltpu.VMEM((APPLIES, WAVES, 2, own // WAVES // 2, width), f32),
+            pltpu.VMEM((APPLIES, WAVES, 2, own // WAVES, width), f32),
+            pltpu.VMEM((APPLIES, WAVES, 2, own // WAVES, width), f32),
+            pltpu.VMEM((own // WAVES, width), f32),
             pltpu.VMEM((own, width), f32),
             pltpu.VMEM((bin_factors.shape[0] // tile, tile, width), bf16),
             pltpu.VMEM((n_tiles, tile, tile), bf16),
@@ -636,6 +659,7 @@
             pltpu.VMEM((part_rows, width), f32),
             pltpu.VMEM((part_rows, width), f32),
             pltpu.VMEM((part_rows, width), f32),
+            pltpu.VMEM((part_rows, width), f32),
             pltpu.VMEM((part_rows // tile, tile, 2 * width), bf16),
             pltpu.VMEM((2, 3, 1, width), f32),
             pltpu.VMEM((window, 1, width), f32),
@@ -644,13 +668,13 @@
             pltpu.VMEM((2, n_bin - 1, 1, width), f32),
             dma((11,)),
             dma((APPLIES,)),
-            dma((APPLIES, n_bin)),
+            dma((APPLIES, WAVES, n_bin)),
             dma((APPLIES,)),
             dma((APPLIES,)),
             dma((APPLIES,)),
             dma((APPLIES,)),
             dma((APPLIES,)),
-            dma((APPLIES, n_bin)),
+            dma((APPLIES, WAVES, n_bin)),
             dma((3,)),
             dma((3,)),
             dma((2, 3)),
@@ -658,7 +682,7 @@
         ],
         compiler_params=pltpu.CompilerParams(collective_id=0, has_side_effects=True),
     )
-    return call(
+    results = call(
         start_factors,
         bin_factors.reshape(-1, tile, width),
         tile_speed[0, 0],
@@ -671,6 +695,12 @@
         face_count[0],
         face_weight[0, 0],
     )
+    held = [pltpu.with_memory_space_constraint(result, pltpu.VMEM) for result in results]
+    out = jax.ShapeDtypeStruct((own, width), f32)
+    finish = pl.pallas_call(
+        finish_kernel, out_shape=(out, out), in_specs=[vmem] * 2, out_specs=(vmem, vmem)
+    )
+    return finish(*held)
 
 
 def solution(mesh):

time: 110 us -> 106 us (0.964)
  Pallas kernels: 107 us -> 105 us
  local copies, waits for them, and re-layouts: 1.23 us -> 0 us
    pallas_call x1, Pallas kernels: 107 us -> 104 us  [shards(): call(start_factors, bin_factors.reshape(-1, tile, width), tile_speed[0, 0...]
    unnamed x2 -> x0, local copies, waits for them, and re-layouts: 1.23 us -> none
where the time goes in v4:
time: 106 us
  Pallas kernels  105 us (99%)
  between operations  1.29 us (1%)
    pallas_call x1, Pallas kernels, shards(): call(start_factors, bin_factors.reshape(-1, tile, width), tile_speed[0, 0...  104 us

profile of v4, /device:TPU:80, one launch (start us, length us, event | category | flops | bytes accessed | tf_op | source)
XLA Modules:
  0.0 106.1 jit_solution(15908550688079872361)
XLA Ops:
  1.3 104.2 %shard_map.122 = (f32[64,128]{1,0:T(8,128)S(1)}, f32[64,128]{1,0:T(8,128)S(1)}) custom-call(f32[64,128]{1,0:T(8,128)} %x0_hbm.1, bf16[8,128,128]{2,1,0:T(8,128)(2,1)} %bitcast.13, bf16[12,128,128]{2,1,0:T(8,128)(2,1)} %bitcast.11, bf16[12,128,128]{2,1,0:T(8,128)(2,1)} %bitcast.12, s32[2,12]{1,0:T(2,128)} %bitcast.17, s32[1,1]{1,0:T(1,128)S(6)} %copy.13.count_hbm, ...), custom_call_target="tpu_custom_call" | custom-call | tf_op jit(solution)/shard_map/pallas_call | solution.py:685
  105.5 0.6 shard_map.123

commit v5 on v4

--- a/solution.py
+++ b/solution.py
@@ -558,19 +558,11 @@
     for wave in range(WAVES):
         mine = block_rows(wave, 0)
         last[wave * wave_rows : (wave + 1) * wave_rows] = scatter_finish(2, wave) + RIDGE * field[2, mine]
-    norm_next, product_next = sums_finish(1)
-    product_next = product_next + RIDGE * norm_next
-    beta = norm_next / norm
-    step_two = norm_next / (product_next - beta * norm_next / step_one)
     residual = field[1, own_slice()]
     image = field[2, own_slice()]
     later = residual - step_one * image
     later_image = image - step_one * last[...]
-    direction = later + beta * residual
-    along = later_image + beta * image
-    sol_ref[...] = field[0, own_slice()] + step_one * residual + step_two * direction
-    res_ref[...] = later - step_two * along
-
+    reached = field[0, own_slice()] + step_one * residual
     pltpu.make_async_copy(rows, rows, setup_send.at[0]).wait()
     pltpu.make_async_copy(rows, rows, setup_send.at[1]).wait()
     pltpu.make_async_copy(face, face, setup_send.at[2]).wait()
@@ -583,8 +575,14 @@
     pltpu.make_async_copy(sums_seg, sums_seg, sums_send.at[0, 0]).wait()
     pltpu.make_async_copy(sums_far, sums_far, sums_send.at[0, 1]).wait()
     pltpu.make_async_copy(sums_all, sums_all, sums_send.at[1, 0]).wait()
-    for turn in range(2):
-        pltpu.make_async_copy(sums_bin.at[turn], sums_bin.at[turn], sums_send.at[turn, 2]).wait()
+    pltpu.make_async_copy(sums_bin.at[0], sums_bin.at[0], sums_send.at[0, 2]).wait()
+    pltpu.make_async_copy(sums_bin.at[1], sums_bin.at[1], sums_send.at[1, 2]).wait()
+    norm_next, product_next = sums_finish(1)
+    product_next = product_next + RIDGE * norm_next
+    beta = norm_next / norm
+    step_two = norm_next / (product_next - beta * norm_next / step_one)
+    sol_ref[...] = reached + step_two * (later + beta * residual)
+    res_ref[...] = later - step_two * (later_image + beta * image)
 
 
 def finish_kernel(sol_in, res_in, sol_ref, res_ref):

time: 106 us -> 106 us (level)
  no operation moved by 1% of the time
where the time goes in v5:
time: 106 us
  Pallas kernels  105 us (99%)
  between operations  1.29 us (1%)
    pallas_call x1, Pallas kernels, shards(): call(start_factors, bin_factors.reshape(-1, tile, width), tile_speed[0, 0...  104 us

profile of v5, /device:TPU:80, one launch (start us, length us, event | category | flops | bytes accessed | tf_op | source)
XLA Modules:
  0.0 106.1 jit_solution(584761574154777255)
XLA Ops:
  1.3 104.2 %shard_map.122 = (f32[64,128]{1,0:T(8,128)S(1)}, f32[64,128]{1,0:T(8,128)S(1)}) custom-call(f32[64,128]{1,0:T(8,128)} %x0_hbm.1, bf16[8,128,128]{2,1,0:T(8,128)(2,1)} %bitcast.13, bf16[12,128,128]{2,1,0:T(8,128)(2,1)} %bitcast.11, bf16[12,128,128]{2,1,0:T(8,128)(2,1)} %bitcast.12, s32[2,12]{1,0:T(2,128)} %bitcast.17, s32[1,1]{1,0:T(1,128)S(6)} %copy.13.count_hbm, ...), custom_call_target="tpu_custom_call" | custom-call | tf_op jit(solution)/shard_map/pallas_call | solution.py:683
  105.4 0.6 shard_map.123
